TPU v7x, 128 devices: a whole 4x4x4 slice. The times are simulated.
128 devices in a mesh: gx: 4 (over y_lo, core), gy: 4 (over x), gz: 8 (over y_hi, z).
Axes of the slice: x: 4, y: 4 (y_hi: 2, y_lo: 2; y = y_hi * 2 + y_lo), z: 4, core: 2. Of those that a mesh axis runs over, the one named last changes fastest.
Arguments:
- right_side: float32 [16, 16, 32, 4, 256], P('gx', 'gy', 'gz'), may hold values from -80 to 80
- bond_blocks: float32 [13, 4, 4, 16, 16, 32], P(None, None, None, 'gx', 'gy', 'gz'), may hold values from -0.012 to 0.012
- bond_open: int32 [13, 16, 16, 32], P(None, 'gx', 'gy', 'gz'), may hold values 0 or 1
- onsite_blocks: float32 [4, 4, 16, 16, 32], P(None, None, 'gx', 'gy', 'gz'), may hold values from -0.012 to 0.012
- orbital_levels: float32 [4, 16, 16, 32], P(None, 'gx', 'gy', 'gz'), may hold values from 1.3 to 2.6
- column_shift: float32 [256], replicated, may hold values from 0.05 to 1
Outputs:
- solution: float32 [16, 16, 32, 4, 256], P('gx', 'gy', 'gz')
- residual: float32 [16, 16, 32, 4, 256], P('gx', 'gy', 'gz')
All inputs are finite; a program needn't handle non-finite values. No bound on the sum of `bond_open` on one device may be relied on, other than what follows from the above.
Results may differ from a plain program's by a relative error of at most 0.0003.
Values sent between devices are 32-bit elements; how exact they have to be, the bound alone decides.
A program may use at most 192 MiB of HBM per device.

v0:
```python
import functools

import jax
import jax.numpy as jnp
from jax import lax
from jax.sharding import Mesh
from jax.sharding import PartitionSpec as P

ITERS = 3
GZ = ("gz_0", "gz_1")
GX = ("gx_0", "gx_1")
GX_GY_GZ = ("gx_0", "gx_1", "gy", "gz_0", "gz_1")


half_offsets = [
    (first, second, third)
    for first in (-1, 0, 1)
    for second in (-1, 0, 1)
    for third in (-1, 0, 1)
    if (first, second, third) > (0, 0, 0)
]


def extended_2(cells, sides, width):
    for axis, dim in sides:
        count = lax.axis_size(axis)
        head = lax.slice_in_dim(cells, 0, width, axis=dim)
        tail = lax.slice_in_dim(cells, cells.shape[dim] - width, cells.shape[dim], axis=dim)
        cells = jnp.concatenate(
            [
                lax.ppermute(tail, axis, [(i, (i + 1) % count) for i in range(count)]),
                cells,
                lax.ppermute(head, axis, [((i + 1) % count, i) for i in range(count)]),
            ],
            axis=dim,
        )
    return cells


def shifted(value, axis, by):
    peers = lax.axis_size(axis)
    return lax.ppermute(value, axis, [(i, (i + by) % peers) for i in range(peers)])


def one_axis_at_a_time(value, axes):
    return functools.reduce(lax.psum, axes, value)


def block_apply(blocks, vector, flipped):
    orbitals = vector.shape[3]
    rows = []
    for out_orb in range(orbitals):
        total = None
        for in_orb in range(orbitals):
            factor = blocks[in_orb, out_orb] if flipped else blocks[out_orb, in_orb]
            term = factor[..., None] * vector[:, :, :, in_orb, :]
            total = term if total is None else total + term
        rows.append(total)
    return jnp.stack(rows, axis=3)


def hop(blocks, vector):
    return block_apply(blocks, vector, False)


def hop_back(blocks, vector):
    return block_apply(blocks, vector, True)


def window(extended, offset, counts, base_first):
    return extended[
        base_first + offset[0] : base_first + offset[0] + counts[0],
        1 + offset[1] : 1 + offset[1] + counts[1],
        1 + offset[2] : 1 + offset[2] + counts[2],
    ]


def outer_layer(extended, dim, upper):
    inner = extended.shape[dim] - 2
    if upper:
        return lax.slice_in_dim(extended, inner + 1, inner + 2, axis=dim)
    return lax.slice_in_dim(extended, 0, 1, axis=dim)


def settle(extended, dim, from_lower, from_upper):
    inner = extended.shape[dim] - 2
    core = lax.slice_in_dim(extended, 1, inner + 1, axis=dim)
    pads_lower = [(0, 0)] * extended.ndim
    pads_upper = [(0, 0)] * extended.ndim
    pads_lower[dim] = (0, inner - 1)
    pads_upper[dim] = (inner - 1, 0)
    return core + jnp.pad(from_lower, pads_lower) + jnp.pad(from_upper, pads_upper)


def settle_first(extended, from_lower):
    inner = extended.shape[0] - 1
    core = extended[:inner]
    pads_lower = [(0, 0)] * extended.ndim
    pads_lower[0] = (0, inner - 1)
    return core + jnp.pad(from_lower, pads_lower)


def per_device(right_side, bond_blocks, bond_open, onsite_blocks, orbital_levels, column_shift):
    coupled = bond_blocks * bond_open[:, None, None].astype(jnp.float32)
    onsite_sym = 0.5 * (onsite_blocks + jnp.swapaxes(onsite_blocks, 0, 1))
    atom_levels = jnp.transpose(orbital_levels, (1, 2, 3, 0))
    counts = right_side.shape[:3]

    def operate(vector):
        result = hop(onsite_sym, vector) + (atom_levels[..., None] + column_shift) * vector
        side = extended_2(vector, (("gy", 1), (GZ, 2)), 1)
        following = shifted(side[0:1], GX, -1)
        extended = jnp.concatenate([side, following], axis=0)
        for bond_index, offset in enumerate(half_offsets):
            result = result + hop(coupled[bond_index], window(extended, offset, counts, 0))
        spilled = jnp.zeros(
            (counts[0] + 1, counts[1] + 2, counts[2] + 2) + vector.shape[3:], jnp.float32
        )
        for bond_index, offset in enumerate(half_offsets):
            placed = (
                (offset[0], 1 - offset[0]),
                (1 + offset[1], 1 - offset[1]),
                (1 + offset[2], 1 - offset[2]),
                (0, 0),
                (0, 0),
            )
            spilled = spilled + jnp.pad(hop_back(coupled[bond_index], vector), placed)
        top_layer = spilled[counts[0] : counts[0] + 1]
        spilled = settle_first(spilled, shifted(top_layer, GX, 1))
        spilled = settle(
            spilled,
            1,
            shifted(outer_layer(spilled, 1, True), "gy", 1),
            shifted(outer_layer(spilled, 1, False), "gy", -1),
        )
        spilled = settle(
            spilled,
            2,
            shifted(outer_layer(spilled, 2, True), GZ, 1),
            shifted(outer_layer(spilled, 2, False), GZ, -1),
        )
        result = result + spilled
        return result

    def two_products(residual, image):
        return (
            one_axis_at_a_time(jnp.sum(residual * residual, axis=(0, 1, 2, 3)), GX_GY_GZ),
            one_axis_at_a_time(jnp.sum(residual * image, axis=(0, 1, 2, 3)), GX_GY_GZ),
        )

    solution = jnp.zeros_like(right_side)
    residual = right_side
    image = operate(residual)
    norm_now, product = two_products(residual, image)
    alpha = norm_now / product
    direction = residual
    along = image
    for iteration in range(ITERS):
        solution = solution + alpha * direction
        residual = residual - alpha * along
        if iteration + 1 < ITERS:
            image = operate(residual)
            norm_next, product = two_products(residual, image)
            ratio = norm_next / norm_now
            alpha = norm_next / (product - ratio * norm_next / alpha)
            direction = residual + ratio * direction
            along = image + ratio * along
            norm_now = norm_next
    return (solution, residual)


def solution(mesh):
    torus = Mesh(
        mesh.devices.reshape(2, 2, mesh.shape["gy"], 2, 4), ("gx_0", "gx_1", "gy", "gz_0", "gz_1")
    )
    return jax.shard_map(
        per_device,
        mesh=torus,
        in_specs=(
            P(GX, "gy", GZ, None, None),
            P(None, None, None, GX, "gy", GZ),
            P(None, GX, "gy", GZ),
            P(None, None, GX, "gy", GZ),
            P(None, GX, "gy", GZ),
            P(),
        ),
        out_specs=(P(GX, "gy", GZ, None, None), P(GX, "gy", GZ, None, None)),
        check_vma=False,
    )
```

profile of v0, /device:TPU:0, one launch (start us, length us, event | category | flops | bytes accessed | tf_op | source)
XLA Modules:
  0.0 346.7 jit_solution(12432175768327176531)
XLA Ops:
  0.6 1.5 fusion.136
  2.2 1.6 collective-permute-start
  4.9 8.4 %slice_reduce_fusion.12 = (f32[4,4,4,4,4]{4,3,2,1,0:T(4,128)S(1)}, f32[4,4,4,4,4]{4,3,2,1,0:T(4,128)S(1)}, f32[4,4,4,4,4]{4,3,2,1,0:T(4,128)S(1)}, f32[4,4,4,4,4...) fusion(f32[13,4,4,4,4,4]{0,5,4,3,2,1:T(4,128)S(1)} %bitcast.456), kind=kLoop, calls=%fused_computation.212 | loop fusion | bytes 106496 | tf_op jit(solution)/shard_map/slice | solution.py:115
  36.1 8.6 %fusion.36 = f32[5,6,6,4,256]{4,3,2,1,0:T(4,128)S(1)} fusion(f32[4,4,4,1,256]{4,3,2,1,0:T(1,128)S(1)} %get-tuple-element.436, f32[4,4,4,1,256]{4,3,2,1,0:T(1,128)S(1)} %get-tuple-element.435, f32[4,4,4,1,256]{4,3,2,1,0:T(1,128)S(1)} %get-tuple-element.434, f32[4,4,4,1,256]{4,3,2,1,0:T(1,128)S(1)} %get-tuple-element.433, ...), kind=kLoop, calls=%fused_computation.126 | loop fusion | flops 44421120 | bytes 4145152 | tf_op jit(solution)/shard_map/add | solution.py:127
  44.9 1.7 collective-permute-start.1
  47.7 1.7 collective-permute-done.1
  49.5 7.0 %collective-permute-start.2 = (f32[4,6,1,4,256]{4,3,2,1,0:T(4,128)S(1)}, f32[4,6,1,4,256]{4,3,2,1,0:T(4,128)S(1)}, u32[]{:S(2)}, u32[]{:S(2)}) collective-permute-start(f32[4,6,1,4,256]{4,3,2,1,0:T(4,128)S(1)} %get-tuple-element.233), channel_id=1, source_target_pairs={{1,0},{2,1},{3,2},{4,3},{5,4},{6,5},{7,6},{0,7},{9,8},{10,9},{11,1... | collective-permute-start | bytes 294920 | tf_op jit(solution)/shard_map/ppermute | solution.py:33
  58.5 3.0 collective-permute-start.7
  61.6 3.2 collective-permute-done.3
  69.6 3.6 %collective-permute-start.9 = (f32[4,4,1,4,256]{4,3,2,1,0:T(4,128)S(1)}, f32[4,4,1,4,256]{4,3,2,1,0:T(4,128)S(1)}, u32[]{:S(2)}, u32[]{:S(2)}) collective-permute-start(f32[4,4,1,4,256]{4,3,2,1,0:T(4,128)S(1)} %get-tuple-element.235), channel_id=1, source_target_pairs={{0,7},{1,0},{2,1},{3,2},{4,3},{5,4},{6,5},{7,6},{8,15},{9,8},{10,9... | collective-permute-start | bytes 196616 | tf_op jit(solution)/shard_map/ppermute | solution.py:42
  87.1 4.0 %multiply_reduce_fusion.4 = (f32[256]{0:T(256)S(1)}, f32[256]{0:T(256)S(1)}, f32[4,4,4,4,256]{4,3,2,1,0:T(4,128)S(1)}) fusion(f32[4,4,4,4,256]{4,3,2,1,0:T(4,128)S(1)} %copy-done, f32[4,4,1,4,256]{4,3,2,1,0:T(4,128)S(1)} %collective-permute-done.9, f32[4,4,1,4,256]{4,3,2,1,0:T(4,128)S(1)} %collective-permute-done.8, f32[4,4,6,4,256]{4,3,2,1,0:T(4,128)S(1)} %fusion.62, ...), kind=kLoop, calls=%fused_computation.291 | loop fusion | flops 4259328 | bytes 4591616 | tf_op jit(solution)/shard_map/reduce_sum | solution.py:148
  91.1 4.9 %all-reduce.68 = (f32[256]{0:T(256)S(1)}, f32[256]{0:T(256)S(1)}) all-reduce(f32[256]{0:T(256)S(1)} %get-tuple-element.20, f32[256]{0:T(256)S(1)} %get-tuple-element.19), channel_id=1, replica_groups=mesh['gx_0'=2,'gx_1'=2,'gy'=4,'gz_0'=2,'gz_1'=4] {'gx_0'}, use_global_device_ids=true, to_apply=%region_1.2 | all-reduce | flops 512 | bytes 4096 | tf_op jit(solution)/shard_map/psum | solution.py:46
  96.0 2.4 all-reduce.65
  98.5 9.8 %all-reduce.59 = (f32[256]{0:T(256)S(1)}, f32[256]{0:T(256)S(1)}) all-reduce(f32[256]{0:T(256)S(1)} %get-tuple-element.43, f32[256]{0:T(256)S(1)} %get-tuple-element.44), channel_id=1, replica_groups=mesh['gx_0'=2,'gx_1'=2,'gy'=4,'gz_0'=2,'gz_1'=4] {'gy'}, use_global_device_ids=true, to_apply=%region_3.4 | all-reduce | flops 512 | bytes 4096 | tf_op jit(solution)/shard_map/psum | solution.py:46
  108.3 6.4 %all-reduce.62 = (f32[256]{0:T(256)S(1)}, f32[256]{0:T(256)S(1)}) all-reduce(f32[256]{0:T(256)S(1)} %get-tuple-element.31, f32[256]{0:T(256)S(1)} %get-tuple-element.32), channel_id=1, replica_groups=mesh['gx_0'=2,'gx_1'=2,'gy'=4,'gz_0'=2,'gz_1'=4] {'gz_0'}, use_global_device_ids=true, to_apply=%region_4.5 | all-reduce | flops 512 | bytes 4096 | tf_op jit(solution)/shard_map/psum | solution.py:46
  114.7 10.6 %all-reduce.56 = (f32[256]{0:T(256)S(1)}, f32[256]{0:T(256)S(1)}) all-reduce(f32[256]{0:T(256)S(1)} %get-tuple-element.37, f32[256]{0:T(256)S(1)} %get-tuple-element.38), channel_id=1, replica_groups=mesh['gx_0'=2,'gx_1'=2,'gy'=4,'gz_0'=2,'gz_1'=4] {'gz_1'}, use_global_device_ids=true, to_apply=%region_5.6 | all-reduce | flops 512 | bytes 4096 | tf_op jit(solution)/shard_map/psum | solution.py:46
  145.8 2.1 collective-permute-start.10
  147.9 1.8 collective-permute-done.11
  150.4 8.6 %fusion.24 = f32[5,6,6,4,256]{4,3,2,1,0:T(4,128)S(1)} fusion(f32[4,4,4,1,256]{4,3,2,1,0:T(1,128)S(1)} %multiply_add_fusion.110, f32[4,4,4,1,256]{4,3,2,1,0:T(1,128)S(1)} %get-tuple-element.367, f32[4,4,4,1,256]{4,3,2,1,0:T(1,128)S(1)} %get-tuple-element.366, f32[4,4,4,1,256]{4,3,2,1,0:T(1,128)S(1)} %get-tuple-element.365, ...), kind=kLoop, calls=%fused_computation.75 | loop fusion | flops 44421120 | bytes 4145152 | tf_op jit(solution)/shard_map/add | solution.py:127
  159.2 3.0 collective-permute-start.12
  163.2 1.6 collective-permute-done.12
  167.1 4.1 %collective-permute-done.13 = f32[4,6,1,4,256]{4,3,2,1,0:T(4,128)S(1)} collective-permute-done((f32[4,6,1,4,256]{4,3,2,1,0:T(4,128)S(1)}, f32[4,6,1,4,256]{4,3,2,1,0:T(4,128)S(1)}, u32[]{:S(2)}, u32[]{:S(2)}) %collective-permute-start.13) | collective-permute-done | bytes 98336 | tf_op jit(solution)/shard_map/ppermute | solution.py:31
  173.7 1.3 collective-permute-start.17
  188.4 3.2 collective-permute-start.19
  193.5 6.4 %collective-permute-done.18 = f32[4,4,1,4,256]{4,3,2,1,0:T(4,128)S(1)} collective-permute-done((f32[4,4,1,4,256]{4,3,2,1,0:T(4,128)S(1)}, f32[4,4,1,4,256]{4,3,2,1,0:T(4,128)S(1)}, u32[]{:S(2)}, u32[]{:S(2)}) %collective-permute-start.18) | collective-permute-done | bytes 65568 | tf_op jit(solution)/shard_map/ppermute | solution.py:42
  199.9 4.0 %multiply_reduce_fusion.2 = (f32[256]{0:T(256)S(1)}, f32[256]{0:T(256)S(1)}, f32[4,4,4,4,256]{4,3,2,1,0:T(4,128)S(1)}) fusion(f32[4,4,4,4,256]{4,3,2,1,0:T(4,128)S(1)} %multiply_subtract_fusion.2, f32[4,4,1,4,256]{4,3,2,1,0:T(4,128)S(1)} %collective-permute-done.19, f32[4,4,1,4,256]{4,3,2,1,0:T(4,128)S(1)} %collective-permute-done.18, ...), kind=kLoop, calls=%fused_computation.288 | loop fusion | flops 4259328 | bytes 4591616 | tf_op jit(solution)/shard_map/reduce_sum | solution.py:148
  203.9 4.9 %all-reduce.67 = (f32[256]{0:T(256)S(1)}, f32[256]{0:T(256)S(1)}) all-reduce(f32[256]{0:T(256)S(1)} %get-tuple-element.18, f32[256]{0:T(256)S(1)} %get-tuple-element.17), channel_id=1, replica_groups=mesh['gx_0'=2,'gx_1'=2,'gy'=4,'gz_0'=2,'gz_1'=4] {'gx_0'}, use_global_device_ids=true, to_apply=%region_13.14 | all-reduce | flops 512 | bytes 4096 | tf_op jit(solution)/shard_map/psum | solution.py:46
  208.8 2.4 all-reduce.64
  211.2 10.1 %all-reduce.58 = (f32[256]{0:T(256)S(1)}, f32[256]{0:T(256)S(1)}) all-reduce(f32[256]{0:T(256)S(1)} %get-tuple-element.41, f32[256]{0:T(256)S(1)} %get-tuple-element.42), channel_id=1, replica_groups=mesh['gx_0'=2,'gx_1'=2,'gy'=4,'gz_0'=2,'gz_1'=4] {'gy'}, use_global_device_ids=true, to_apply=%region_15.16 | all-reduce | flops 512 | bytes 4096 | tf_op jit(solution)/shard_map/psum | solution.py:46
  221.4 6.4 %all-reduce.61 = (f32[256]{0:T(256)S(1)}, f32[256]{0:T(256)S(1)}) all-reduce(f32[256]{0:T(256)S(1)} %get-tuple-element.29, f32[256]{0:T(256)S(1)} %get-tuple-element.30), channel_id=1, replica_groups=mesh['gx_0'=2,'gx_1'=2,'gy'=4,'gz_0'=2,'gz_1'=4] {'gz_0'}, use_global_device_ids=true, to_apply=%region_16.17 | all-reduce | flops 512 | bytes 4096 | tf_op jit(solution)/shard_map/psum | solution.py:46
  227.8 7.7 %all-reduce.55 = (f32[256]{0:T(256)S(1)}, f32[256]{0:T(256)S(1)}) all-reduce(f32[256]{0:T(256)S(1)} %get-tuple-element.35, f32[256]{0:T(256)S(1)} %get-tuple-element.36), channel_id=1, replica_groups=mesh['gx_0'=2,'gx_1'=2,'gy'=4,'gz_0'=2,'gz_1'=4] {'gz_1'}, use_global_device_ids=true, to_apply=%region_17.18 | all-reduce | flops 512 | bytes 4096 | tf_op jit(solution)/shard_map/psum | solution.py:46
  255.9 2.1 collective-permute-start.20
  257.9 1.8 collective-permute-done.21
  260.5 8.6 %fusion.12 = f32[5,6,6,4,256]{4,3,2,1,0:T(4,128)S(1)} fusion(f32[4,4,4,1,256]{4,3,2,1,0:T(1,128)S(1)} %multiply_add_fusion.2, f32[4,4,4,1,256]{4,3,2,1,0:T(1,128)S(1)} %get-tuple-element.305, f32[4,4,4,1,256]{4,3,2,1,0:T(1,128)S(1)} %get-tuple-element.304, f32[4,4,4,1,256]{4,3,2,1,0:T(1,128)S(1)} %get-tuple-element.303, ...), kind=kLoop, calls=%fused_computation.24 | loop fusion | flops 44421120 | bytes 4145152 | tf_op jit(solution)/shard_map/add | solution.py:127
  269.3 3.4 collective-permute-start.22
  273.7 1.2 collective-permute-done.22
  277.2 3.9 %collective-permute-done.23 = f32[4,6,1,4,256]{4,3,2,1,0:T(4,128)S(1)} collective-permute-done((f32[4,6,1,4,256]{4,3,2,1,0:T(4,128)S(1)}, f32[4,6,1,4,256]{4,3,2,1,0:T(4,128)S(1)}, u32[]{:S(2)}, u32[]{:S(2)}) %collective-permute-start.23) | collective-permute-done | bytes 98336 | tf_op jit(solution)/shard_map/ppermute | solution.py:31
  283.6 1.3 collective-permute-start.27
  298.6 3.2 collective-permute-start.29
  302.5 1.2 collective-permute-done.29
  303.7 6.0 %collective-permute-done.28 = f32[4,4,1,4,256]{4,3,2,1,0:T(4,128)S(1)} collective-permute-done((f32[4,4,1,4,256]{4,3,2,1,0:T(4,128)S(1)}, f32[4,4,1,4,256]{4,3,2,1,0:T(4,128)S(1)}, u32[]{:S(2)}, u32[]{:S(2)}) %collective-permute-start.28) | collective-permute-done | bytes 65568 | tf_op jit(solution)/shard_map/ppermute | solution.py:42
  309.6 4.0 %multiply_reduce_fusion = (f32[256]{0:T(256)S(1)}, f32[256]{0:T(256)S(1)}, f32[4,4,4,4,256]{4,3,2,1,0:T(4,128)S(1)}) fusion(f32[4,4,4,4,256]{4,3,2,1,0:T(4,128)S(1)} %multiply_subtract_fusion.1, f32[4,4,1,4,256]{4,3,2,1,0:T(4,128)S(1)} %collective-permute-done.29, f32[4,4,1,4,256]{4,3,2,1,0:T(4,128)S(1)} %collective-permute-done.28, ...), kind=kLoop, calls=%fused_computation.284 | loop fusion | flops 4259328 | bytes 4591616 | tf_op jit(solution)/shard_map/reduce_sum | solution.py:148
  313.6 4.9 %all-reduce.66 = (f32[256]{0:T(256)S(1)}, f32[256]{0:T(256)S(1)}) all-reduce(f32[256]{0:T(256)S(1)} %get-tuple-element.16, f32[256]{0:T(256)S(1)} %get-tuple-element.15), channel_id=1, replica_groups=mesh['gx_0'=2,'gx_1'=2,'gy'=4,'gz_0'=2,'gz_1'=4] {'gx_0'}, use_global_device_ids=true, to_apply=%region_25.26 | all-reduce | flops 512 | bytes 4096 | tf_op jit(solution)/shard_map/psum | solution.py:46
  318.5 2.4 all-reduce.63
  321.0 10.1 %all-reduce.57 = (f32[256]{0:T(256)S(1)}, f32[256]{0:T(256)S(1)}) all-reduce(f32[256]{0:T(256)S(1)} %get-tuple-element.39, f32[256]{0:T(256)S(1)} %get-tuple-element.40), channel_id=1, replica_groups=mesh['gx_0'=2,'gx_1'=2,'gy'=4,'gz_0'=2,'gz_1'=4] {'gy'}, use_global_device_ids=true, to_apply=%region_27.28 | all-reduce | flops 512 | bytes 4096 | tf_op jit(solution)/shard_map/psum | solution.py:46
  331.1 6.4 %all-reduce.60 = (f32[256]{0:T(256)S(1)}, f32[256]{0:T(256)S(1)}) all-reduce(f32[256]{0:T(256)S(1)} %get-tuple-element.27, f32[256]{0:T(256)S(1)} %get-tuple-element.28), channel_id=1, replica_groups=mesh['gx_0'=2,'gx_1'=2,'gy'=4,'gz_0'=2,'gz_1'=4] {'gz_0'}, use_global_device_ids=true, to_apply=%region_28.29 | all-reduce | flops 512 | bytes 4096 | tf_op jit(solution)/shard_map/psum | solution.py:46
  337.5 7.7 %all-reduce.54 = (f32[256]{0:T(256)S(1)}, f32[256]{0:T(256)S(1)}) all-reduce(f32[256]{0:T(256)S(1)} %get-tuple-element.33, f32[256]{0:T(256)S(1)} %get-tuple-element.34), channel_id=1, replica_groups=mesh['gx_0'=2,'gx_1'=2,'gy'=4,'gz_0'=2,'gz_1'=4] {'gz_1'}, use_global_device_ids=true, to_apply=%region_29.30 | all-reduce | flops 512 | bytes 4096 | tf_op jit(solution)/shard_map/psum | solution.py:46
  345.3 1.2 multiply_subtract_fusion
  (326 shorter events, 127.6 us)
Async XLA Ops:
  0.6 3.2 copy-start.34
  2.2 44.6 %collective-permute-start = (f32[4,1,4,4,256]{4,3,2,1,0:T(4,128)}, f32[4,1,4,4,256]{4,3,2,1,0:T(4,128)}, u32[]{:S(2)}, u32[]{:S(2)}) collective-permute-start(f32[4,1,4,4,256]{4,3,2,1,0:T(4,128)} %get-tuple-element.388), channel_id=1, source_target_pairs={{0,8},{8,16},{16,24},{24,0},{1,9},{9,17},{17,25},{25,1},{2,10},{10... | collective-permute-start | bytes 196616 | tf_op jit(solution)/shard_map/ppermute | solution.py:31
  14.5 18.5 %copy-start.25 = (f32[4,4,4]{2,1,0:T(4,128)}, f32[4,4,4]{2,1,0:T(4,128)S(1)}, u32[]{:S(2)}) copy-start(f32[4,4,4]{2,1,0:T(4,128)S(1)} %get-tuple-element.438) | copy-start | bytes 772
  14.6 18.5 %copy-start.27 = (f32[4,4,4]{2,1,0:T(4,128)}, f32[4,4,4]{2,1,0:T(4,128)S(1)}, u32[]{:S(2)}) copy-start(f32[4,4,4]{2,1,0:T(4,128)S(1)} %get-tuple-element.439) | copy-start | bytes 772
  14.6 18.5 %copy-start.29 = (f32[4,4,4]{2,1,0:T(4,128)}, f32[4,4,4]{2,1,0:T(4,128)S(1)}, u32[]{:S(2)}) copy-start(f32[4,4,4]{2,1,0:T(4,128)S(1)} %get-tuple-element.440) | copy-start | bytes 772
  14.6 18.5 %copy-start.31 = (f32[4,4,4]{2,1,0:T(4,128)}, f32[4,4,4]{2,1,0:T(4,128)S(1)}, u32[]{:S(2)}) copy-start(f32[4,4,4]{2,1,0:T(4,128)S(1)} %get-tuple-element.441) | copy-start | bytes 772
  14.6 19.2 %copy-start.17 = (f32[4,4,4]{2,1,0:T(4,128)}, f32[4,4,4]{2,1,0:T(4,128)S(1)}, u32[]{:S(2)}) copy-start(f32[4,4,4]{2,1,0:T(4,128)S(1)} %get-tuple-element.442) | copy-start | bytes 772
  14.6 19.2 %copy-start.19 = (f32[4,4,4]{2,1,0:T(4,128)}, f32[4,4,4]{2,1,0:T(4,128)S(1)}, u32[]{:S(2)}) copy-start(f32[4,4,4]{2,1,0:T(4,128)S(1)} %get-tuple-element.443) | copy-start | bytes 772
  14.6 19.2 %copy-start.21 = (f32[4,4,4]{2,1,0:T(4,128)}, f32[4,4,4]{2,1,0:T(4,128)S(1)}, u32[]{:S(2)}) copy-start(f32[4,4,4]{2,1,0:T(4,128)S(1)} %get-tuple-element.444) | copy-start | bytes 772
  14.6 19.2 %copy-start.23 = (f32[4,4,4]{2,1,0:T(4,128)}, f32[4,4,4]{2,1,0:T(4,128)S(1)}, u32[]{:S(2)}) copy-start(f32[4,4,4]{2,1,0:T(4,128)S(1)} %get-tuple-element.445) | copy-start | bytes 772
  14.6 20.0 %copy-start.9 = (f32[4,4,4]{2,1,0:T(4,128)}, f32[4,4,4]{2,1,0:T(4,128)S(1)}, u32[]{:S(2)}) copy-start(f32[4,4,4]{2,1,0:T(4,128)S(1)} %get-tuple-element.446) | copy-start | bytes 772
  14.6 20.0 %copy-start.11 = (f32[4,4,4]{2,1,0:T(4,128)}, f32[4,4,4]{2,1,0:T(4,128)S(1)}, u32[]{:S(2)}) copy-start(f32[4,4,4]{2,1,0:T(4,128)S(1)} %get-tuple-element.447) | copy-start | bytes 772
  14.6 20.0 %copy-start.13 = (f32[4,4,4]{2,1,0:T(4,128)}, f32[4,4,4]{2,1,0:T(4,128)S(1)}, u32[]{:S(2)}) copy-start(f32[4,4,4]{2,1,0:T(4,128)S(1)} %get-tuple-element.448) | copy-start | bytes 772
  14.7 20.0 %copy-start.15 = (f32[4,4,4]{2,1,0:T(4,128)}, f32[4,4,4]{2,1,0:T(4,128)S(1)}, u32[]{:S(2)}) copy-start(f32[4,4,4]{2,1,0:T(4,128)S(1)} %get-tuple-element.449) | copy-start | bytes 772
  14.7 20.7 %copy-start.1 = (f32[4,4,4]{2,1,0:T(4,128)}, f32[4,4,4]{2,1,0:T(4,128)S(1)}, u32[]{:S(2)}) copy-start(f32[4,4,4]{2,1,0:T(4,128)S(1)} %get-tuple-element.437) | copy-start | bytes 772
  14.7 20.7 %copy-start.3 = (f32[4,4,4]{2,1,0:T(4,128)}, f32[4,4,4]{2,1,0:T(4,128)S(1)}, u32[]{:S(2)}) copy-start(f32[4,4,4]{2,1,0:T(4,128)S(1)} %get-tuple-element.450) | copy-start | bytes 772
  14.7 20.7 %copy-start.5 = (f32[4,4,4]{2,1,0:T(4,128)}, f32[4,4,4]{2,1,0:T(4,128)S(1)}, u32[]{:S(2)}) copy-start(f32[4,4,4]{2,1,0:T(4,128)S(1)} %get-tuple-element.451) | copy-start | bytes 772
  14.7 20.7 %copy-start.7 = (f32[4,4,4]{2,1,0:T(4,128)}, f32[4,4,4]{2,1,0:T(4,128)S(1)}, u32[]{:S(2)}) copy-start(f32[4,4,4]{2,1,0:T(4,128)S(1)} %get-tuple-element.452) | copy-start | bytes 772
  44.8 1.8 copy-start.35
  44.8 13.6 %collective-permute-start.5 = (f32[1,6,6,4,256]{4,3,2,1,0:T(4,128)S(1)}, f32[1,6,6,4,256]{4,3,2,1,0:T(4,128)S(1)}, u32[]{:S(2)}, u32[]{:S(2)}) collective-permute-start(f32[1,6,6,4,256]{4,3,2,1,0:T(4,128)S(1)} %slice.1794), channel_id=1, source_target_pairs={{0,32},{32,64},{64,96},{96,0},{1,33},{33,65},{65,97},{97,1},{2,34}... | collective-permute-start | bytes 442376 | tf_op jit(solution)/shard_map/ppermute | solution.py:42
  44.9 4.6 %collective-permute-start.1 = (f32[4,1,4,4,256]{4,3,2,1,0:T(4,128)}, f32[4,1,4,4,256]{4,3,2,1,0:T(4,128)S(1)}, u32[]{:S(2)}, u32[]{:S(2)}) collective-permute-start(f32[4,1,4,4,256]{4,3,2,1,0:T(4,128)} %get-tuple-element.387), channel_id=1, source_target_pairs={{8,0},{16,8},{24,16},{0,24},{9,1},{17,9},{25,17},{1,25},{10,2},{18... | collective-permute-start | bytes 196616 | tf_op jit(solution)/shard_map/ppermute | solution.py:33
  49.5 12.0 %collective-permute-start.2 = (f32[4,6,1,4,256]{4,3,2,1,0:T(4,128)S(1)}, f32[4,6,1,4,256]{4,3,2,1,0:T(4,128)S(1)}, u32[]{:S(2)}, u32[]{:S(2)}) collective-permute-start(f32[4,6,1,4,256]{4,3,2,1,0:T(4,128)S(1)} %get-tuple-element.233), channel_id=1, source_target_pairs={{1,0},{2,1},{3,2},{4,3},{5,4},{6,5},{7,6},{0,7},{9,8},{10,9},{11,1... | collective-permute-start | bytes 294920 | tf_op jit(solution)/shard_map/ppermute | solution.py:33
  56.6 8.2 %collective-permute-start.3 = (f32[4,6,1,4,256]{4,3,2,1,0:T(4,128)S(1)}, f32[4,6,1,4,256]{4,3,2,1,0:T(4,128)S(1)}, u32[]{:S(2)}, u32[]{:S(2)}) collective-permute-start(f32[4,6,1,4,256]{4,3,2,1,0:T(4,128)S(1)} %get-tuple-element.232), channel_id=1, source_target_pairs={{0,1},{1,2},{2,3},{3,4},{4,5},{5,6},{6,7},{7,0},{8,9},{9,10},{10,1... | collective-permute-start | bytes 294920 | tf_op jit(solution)/shard_map/ppermute | solution.py:31
  58.5 10.9 %collective-permute-start.7 = (f32[4,1,6,4,256]{4,3,2,1,0:T(4,128)S(1)}, f32[4,1,6,4,256]{4,3,2,1,0:T(4,128)S(1)}, u32[]{:S(2)}, u32[]{:S(2)}) collective-permute-start(f32[4,1,6,4,256]{4,3,2,1,0:T(4,128)S(1)} %get-tuple-element.207), channel_id=1, source_target_pairs={{0,24},{8,0},{16,8},{24,16},{1,25},{9,1},{17,9},{25,17},{2,26},{10... | collective-permute-start | bytes 294920 | tf_op jit(solution)/shard_map/ppermute | solution.py:42
  61.6 7.9 %collective-permute-start.6 = (f32[4,1,6,4,256]{4,3,2,1,0:T(4,128)S(1)}, f32[4,1,6,4,256]{4,3,2,1,0:T(4,128)S(1)}, u32[]{:S(2)}, u32[]{:S(2)}) collective-permute-start(f32[4,1,6,4,256]{4,3,2,1,0:T(4,128)S(1)} %get-tuple-element.206), channel_id=1, source_target_pairs={{0,8},{8,16},{16,24},{24,0},{1,9},{9,17},{17,25},{25,1},{2,10},{10... | collective-permute-start | bytes 294920 | tf_op jit(solution)/shard_map/ppermute | solution.py:42
  64.8 8.4 %collective-permute-start.4 = (f32[1,6,6,4,256]{4,3,2,1,0:T(4,128)S(1)}, f32[1,6,6,4,256]{4,3,2,1,0:T(4,128)S(1)}, u32[]{:S(2)}, u32[]{:S(2)}) collective-permute-start(f32[1,6,6,4,256]{4,3,2,1,0:T(4,128)S(1)} %pad_maximum_fusion.13), channel_id=1, source_target_pairs={{0,96},{32,0},{64,32},{96,64},{1,97},{33,1},{65,33},{97,65},{2,98}... | collective-permute-start | bytes 442376 | tf_op jit(solution)/shard_map/ppermute | solution.py:42
  69.6 16.8 %collective-permute-start.9 = (f32[4,4,1,4,256]{4,3,2,1,0:T(4,128)S(1)}, f32[4,4,1,4,256]{4,3,2,1,0:T(4,128)S(1)}, u32[]{:S(2)}, u32[]{:S(2)}) collective-permute-start(f32[4,4,1,4,256]{4,3,2,1,0:T(4,128)S(1)} %get-tuple-element.235), channel_id=1, source_target_pairs={{0,7},{1,0},{2,1},{3,2},{4,3},{5,4},{6,5},{7,6},{8,15},{9,8},{10,9... | collective-permute-start | bytes 196616 | tf_op jit(solution)/shard_map/ppermute | solution.py:42
  73.2 13.2 %collective-permute-start.8 = (f32[4,4,1,4,256]{4,3,2,1,0:T(4,128)S(1)}, f32[4,4,1,4,256]{4,3,2,1,0:T(4,128)S(1)}, u32[]{:S(2)}, u32[]{:S(2)}) collective-permute-start(f32[4,4,1,4,256]{4,3,2,1,0:T(4,128)S(1)} %get-tuple-element.234), channel_id=1, source_target_pairs={{0,1},{1,2},{2,3},{3,4},{4,5},{5,6},{6,7},{7,0},{8,9},{9,10},{10,1... | collective-permute-start | bytes 196616 | tf_op jit(solution)/shard_map/ppermute | solution.py:42
  145.3 4.3 %collective-permute-start.11 = (f32[4,1,4,4,256]{4,3,2,1,0:T(4,128)S(1)}, f32[4,1,4,4,256]{4,3,2,1,0:T(4,128)S(1)}, u32[]{:S(2)}, u32[]{:S(2)}) collective-permute-start(f32[4,1,4,4,256]{4,3,2,1,0:T(4,128)S(1)} %get-tuple-element.321), channel_id=1, source_target_pairs={{8,0},{16,8},{24,16},{0,24},{9,1},{17,9},{25,17},{1,25},{10,2},{18... | collective-permute-start | bytes 196616 | tf_op jit(solution)/shard_map/ppermute | solution.py:33
  145.8 13.4 %collective-permute-start.10 = (f32[4,1,4,4,256]{4,3,2,1,0:T(4,128)S(1)}, f32[4,1,4,4,256]{4,3,2,1,0:T(4,128)S(1)}, u32[]{:S(2)}, u32[]{:S(2)}) collective-permute-start(f32[4,1,4,4,256]{4,3,2,1,0:T(4,128)S(1)} %get-tuple-element.320), channel_id=1, source_target_pairs={{0,8},{8,16},{16,24},{24,0},{1,9},{9,17},{17,25},{25,1},{2,10},{10... | collective-permute-start | bytes 196616 | tf_op jit(solution)/shard_map/ppermute | solution.py:31
  159.1 14.5 %collective-permute-start.15 = (f32[1,6,6,4,256]{4,3,2,1,0:T(4,128)S(1)}, f32[1,6,6,4,256]{4,3,2,1,0:T(4,128)S(1)}, u32[]{:S(2)}, u32[]{:S(2)}) collective-permute-start(f32[1,6,6,4,256]{4,3,2,1,0:T(4,128)S(1)} %slice.1852), channel_id=1, source_target_pairs={{0,32},{32,64},{64,96},{96,0},{1,33},{33,65},{65,97},{97,1},{2,34}... | collective-permute-start | bytes 442376 | tf_op jit(solution)/shard_map/ppermute | solution.py:42
  159.2 5.6 %collective-permute-start.12 = (f32[4,6,1,4,256]{4,3,2,1,0:T(4,128)S(1)}, f32[4,6,1,4,256]{4,3,2,1,0:T(4,128)S(1)}, u32[]{:S(2)}, u32[]{:S(2)}) collective-permute-start(f32[4,6,1,4,256]{4,3,2,1,0:T(4,128)S(1)} %get-tuple-element.229), channel_id=1, source_target_pairs={{1,0},{2,1},{3,2},{4,3},{5,4},{6,5},{7,6},{0,7},{9,8},{10,9},{11,1... | collective-permute-start | bytes 294920 | tf_op jit(solution)/shard_map/ppermute | solution.py:33
  162.2 9.0 %collective-permute-start.13 = (f32[4,6,1,4,256]{4,3,2,1,0:T(4,128)S(1)}, f32[4,6,1,4,256]{4,3,2,1,0:T(4,128)S(1)}, u32[]{:S(2)}, u32[]{:S(2)}) collective-permute-start(f32[4,6,1,4,256]{4,3,2,1,0:T(4,128)S(1)} %get-tuple-element.228), channel_id=1, source_target_pairs={{0,1},{1,2},{2,3},{3,4},{4,5},{5,6},{6,7},{7,0},{8,9},{9,10},{10,1... | collective-permute-start | bytes 294920 | tf_op jit(solution)/shard_map/ppermute | solution.py:31
  171.2 4.6 %collective-permute-start.14 = (f32[1,6,6,4,256]{4,3,2,1,0:T(4,128)S(1)}, f32[1,6,6,4,256]{4,3,2,1,0:T(4,128)S(1)}, u32[]{:S(2)}, u32[]{:S(2)}) collective-permute-start(f32[1,6,6,4,256]{4,3,2,1,0:T(4,128)S(1)} %pad_maximum_fusion.9), channel_id=1, source_target_pairs={{0,96},{32,0},{64,32},{96,64},{1,97},{33,1},{65,33},{97,65},{2,98}... | collective-permute-start | bytes 442376 | tf_op jit(solution)/shard_map/ppermute | solution.py:42
  173.7 14.6 %collective-permute-start.17 = (f32[4,1,6,4,256]{4,3,2,1,0:T(4,128)S(1)}, f32[4,1,6,4,256]{4,3,2,1,0:T(4,128)S(1)}, u32[]{:S(2)}, u32[]{:S(2)}) collective-permute-start(f32[4,1,6,4,256]{4,3,2,1,0:T(4,128)S(1)} %get-tuple-element.205), channel_id=1, source_target_pairs={{0,24},{8,0},{16,8},{24,16},{1,25},{9,1},{17,9},{25,17},{2,26},{10... | collective-permute-start | bytes 294920 | tf_op jit(solution)/shard_map/ppermute | solution.py:42
  175.0 13.3 %collective-permute-start.16 = (f32[4,1,6,4,256]{4,3,2,1,0:T(4,128)S(1)}, f32[4,1,6,4,256]{4,3,2,1,0:T(4,128)S(1)}, u32[]{:S(2)}, u32[]{:S(2)}) collective-permute-start(f32[4,1,6,4,256]{4,3,2,1,0:T(4,128)S(1)} %get-tuple-element.204), channel_id=1, source_target_pairs={{0,8},{8,16},{16,24},{24,0},{1,9},{9,17},{17,25},{25,1},{2,10},{10... | collective-permute-start | bytes 294920 | tf_op jit(solution)/shard_map/ppermute | solution.py:42
  188.4 5.1 %collective-permute-start.19 = (f32[4,4,1,4,256]{4,3,2,1,0:T(4,128)S(1)}, f32[4,4,1,4,256]{4,3,2,1,0:T(4,128)S(1)}, u32[]{:S(2)}, u32[]{:S(2)}) collective-permute-start(f32[4,4,1,4,256]{4,3,2,1,0:T(4,128)S(1)} %get-tuple-element.231), channel_id=1, source_target_pairs={{0,7},{1,0},{2,1},{3,2},{4,3},{5,4},{6,5},{7,6},{8,15},{9,8},{10,9... | collective-permute-start | bytes 196616 | tf_op jit(solution)/shard_map/ppermute | solution.py:42
  191.6 8.3 %collective-permute-start.18 = (f32[4,4,1,4,256]{4,3,2,1,0:T(4,128)S(1)}, f32[4,4,1,4,256]{4,3,2,1,0:T(4,128)S(1)}, u32[]{:S(2)}, u32[]{:S(2)}) collective-permute-start(f32[4,4,1,4,256]{4,3,2,1,0:T(4,128)S(1)} %get-tuple-element.230), channel_id=1, source_target_pairs={{0,1},{1,2},{2,3},{3,4},{4,5},{5,6},{6,7},{7,0},{8,9},{9,10},{10,1... | collective-permute-start | bytes 196616 | tf_op jit(solution)/shard_map/ppermute | solution.py:42
  255.3 4.5 %collective-permute-start.21 = (f32[4,1,4,4,256]{4,3,2,1,0:T(4,128)S(1)}, f32[4,1,4,4,256]{4,3,2,1,0:T(4,128)S(1)}, u32[]{:S(2)}, u32[]{:S(2)}) collective-permute-start(f32[4,1,4,4,256]{4,3,2,1,0:T(4,128)S(1)} %get-tuple-element.259), channel_id=1, source_target_pairs={{8,0},{16,8},{24,16},{0,24},{9,1},{17,9},{25,17},{1,25},{10,2},{18... | collective-permute-start | bytes 196616 | tf_op jit(solution)/shard_map/ppermute | solution.py:33
  255.9 13.4 %collective-permute-start.20 = (f32[4,1,4,4,256]{4,3,2,1,0:T(4,128)S(1)}, f32[4,1,4,4,256]{4,3,2,1,0:T(4,128)S(1)}, u32[]{:S(2)}, u32[]{:S(2)}) collective-permute-start(f32[4,1,4,4,256]{4,3,2,1,0:T(4,128)S(1)} %get-tuple-element.258), channel_id=1, source_target_pairs={{0,8},{8,16},{16,24},{24,0},{1,9},{9,17},{17,25},{25,1},{2,10},{10... | collective-permute-start | bytes 196616 | tf_op jit(solution)/shard_map/ppermute | solution.py:31
  269.2 14.3 %collective-permute-start.25 = (f32[1,6,6,4,256]{4,3,2,1,0:T(4,128)S(1)}, f32[1,6,6,4,256]{4,3,2,1,0:T(4,128)S(1)}, u32[]{:S(2)}, u32[]{:S(2)}) collective-permute-start(f32[1,6,6,4,256]{4,3,2,1,0:T(4,128)S(1)} %slice.1910), channel_id=1, source_target_pairs={{0,32},{32,64},{64,96},{96,0},{1,33},{33,65},{65,97},{97,1},{2,34}... | collective-permute-start | bytes 442376 | tf_op jit(solution)/shard_map/ppermute | solution.py:42
  269.3 5.6 %collective-permute-start.22 = (f32[4,6,1,4,256]{4,3,2,1,0:T(4,128)S(1)}, f32[4,6,1,4,256]{4,3,2,1,0:T(4,128)S(1)}, u32[]{:S(2)}, u32[]{:S(2)}) collective-permute-start(f32[4,6,1,4,256]{4,3,2,1,0:T(4,128)S(1)} %get-tuple-element.225), channel_id=1, source_target_pairs={{1,0},{2,1},{3,2},{4,3},{5,4},{6,5},{7,6},{0,7},{9,8},{10,9},{11,1... | collective-permute-start | bytes 294920 | tf_op jit(solution)/shard_map/ppermute | solution.py:33
  272.7 8.4 %collective-permute-start.23 = (f32[4,6,1,4,256]{4,3,2,1,0:T(4,128)S(1)}, f32[4,6,1,4,256]{4,3,2,1,0:T(4,128)S(1)}, u32[]{:S(2)}, u32[]{:S(2)}) collective-permute-start(f32[4,6,1,4,256]{4,3,2,1,0:T(4,128)S(1)} %get-tuple-element.224), channel_id=1, source_target_pairs={{0,1},{1,2},{2,3},{3,4},{4,5},{5,6},{6,7},{7,0},{8,9},{9,10},{10,1... | collective-permute-start | bytes 294920 | tf_op jit(solution)/shard_map/ppermute | solution.py:31
  281.2 4.8 %collective-permute-start.24 = (f32[1,6,6,4,256]{4,3,2,1,0:T(4,128)S(1)}, f32[1,6,6,4,256]{4,3,2,1,0:T(4,128)S(1)}, u32[]{:S(2)}, u32[]{:S(2)}) collective-permute-start(f32[1,6,6,4,256]{4,3,2,1,0:T(4,128)S(1)} %pad_maximum_fusion.5), channel_id=1, source_target_pairs={{0,96},{32,0},{64,32},{96,64},{1,97},{33,1},{65,33},{97,65},{2,98}... | collective-permute-start | bytes 442376 | tf_op jit(solution)/shard_map/ppermute | solution.py:42
  283.6 14.8 %collective-permute-start.27 = (f32[4,1,6,4,256]{4,3,2,1,0:T(4,128)S(1)}, f32[4,1,6,4,256]{4,3,2,1,0:T(4,128)S(1)}, u32[]{:S(2)}, u32[]{:S(2)}) collective-permute-start(f32[4,1,6,4,256]{4,3,2,1,0:T(4,128)S(1)} %get-tuple-element.203), channel_id=1, source_target_pairs={{0,24},{8,0},{16,8},{24,16},{1,25},{9,1},{17,9},{25,17},{2,26},{10... | collective-permute-start | bytes 294920 | tf_op jit(solution)/shard_map/ppermute | solution.py:42
  284.9 13.5 %collective-permute-start.26 = (f32[4,1,6,4,256]{4,3,2,1,0:T(4,128)S(1)}, f32[4,1,6,4,256]{4,3,2,1,0:T(4,128)S(1)}, u32[]{:S(2)}, u32[]{:S(2)}) collective-permute-start(f32[4,1,6,4,256]{4,3,2,1,0:T(4,128)S(1)} %get-tuple-element.202), channel_id=1, source_target_pairs={{0,8},{8,16},{16,24},{24,0},{1,9},{9,17},{17,25},{25,1},{2,10},{10... | collective-permute-start | bytes 294920 | tf_op jit(solution)/shard_map/ppermute | solution.py:42
  298.6 5.1 %collective-permute-start.29 = (f32[4,4,1,4,256]{4,3,2,1,0:T(4,128)S(1)}, f32[4,4,1,4,256]{4,3,2,1,0:T(4,128)S(1)}, u32[]{:S(2)}, u32[]{:S(2)}) collective-permute-start(f32[4,4,1,4,256]{4,3,2,1,0:T(4,128)S(1)} %get-tuple-element.227), channel_id=1, source_target_pairs={{0,7},{1,0},{2,1},{3,2},{4,3},{5,4},{6,5},{7,6},{8,15},{9,8},{10,9... | collective-permute-start | bytes 196616 | tf_op jit(solution)/shard_map/ppermute | solution.py:42
  301.8 7.9 %collective-permute-start.28 = (f32[4,4,1,4,256]{4,3,2,1,0:T(4,128)S(1)}, f32[4,4,1,4,256]{4,3,2,1,0:T(4,128)S(1)}, u32[]{:S(2)}, u32[]{:S(2)}) collective-permute-start(f32[4,4,1,4,256]{4,3,2,1,0:T(4,128)S(1)} %get-tuple-element.226), channel_id=1, source_target_pairs={{0,1},{1,2},{2,3},{3,4},{4,5},{5,6},{6,7},{7,0},{8,9},{9,10},{10,1... | collective-permute-start | bytes 196616 | tf_op jit(solution)/shard_map/ppermute | solution.py:42
  (19 other events, 14.9 us)
where the time goes:
time: 353 us; the launch traced here: 347 us
  other arithmetic  159 us (45%)
  blocking collectives  97.5 us (28%)
  starting transfers between devices  39.4 us (11%)
  waiting for transfers between devices  33.8 us (10%)
  local copies, waits for them, and re-layouts  13.9 us (4%)
    add x162, other arithmetic, block_apply(): total = term if total is None else total + term  117 us
    psum x15, blocking collectives, one_axis_at_a_time(): return functools.reduce(lax.psum, axes, value)  97.5 us
    add x3, other arithmetic, operate(): spilled = spilled + jnp.pad(hop_back(coupled[bond_index], vector), placed)  25.9 us
    ppermute x18, starting transfers between devices, shifted(): lax.ppermute(value, axis, [(i, (i + by) % peers) for i in range(peers)])  18.3 us
    ppermute x6, starting transfers between devices, extended_2(): lax.ppermute(head, axis, [((i + 1) % count, i) for i in range(count)])  15.4 us
    ppermute x18, waiting for transfers between devices, shifted(): lax.ppermute(value, axis, [(i, (i + by) % peers) for i in range(peers)])  14.3 us
    reduce_sum x3, other arithmetic, two_products(): jnp.sum(residual * image, axis=(0, 1, 2, 3))  11.9 us
    ppermute x6, waiting for transfers between devices, extended_2(): lax.ppermute(tail, axis, [(i, (i + 1) % count) for i in range(count)])  11.2 us
  transfers between devices with their start and end apart: 30, of which 12 were waited for; matrix products, arithmetic and copies ran while one was open for 34% of the time, Pallas kernels for 0%

commit v1 on v0

v1 whole, which is shorter than its diff:
```python
import functools

import jax
import jax.numpy as jnp
from jax import lax
from jax.experimental import pallas as pl
from jax.experimental.pallas import tpu as pltpu
from jax.sharding import PartitionSpec as P

f32 = jnp.float32
bf16 = jnp.bfloat16

CENTRE = 1.95
GAMMA1 = 0.65 * 0.65 / 3.0
GAMMA2 = 0.65 * 0.65 * 4.0 / 15.0

half_offsets = [
    (first, second, third)
    for first in (-1, 0, 1)
    for second in (-1, 0, 1)
    for third in (-1, 0, 1)
    if (first, second, third) > (0, 0, 0)
]
directions = sorted(
    [
        (dx, dy, dz)
        for dx in (-1, 0, 1)
        for dy in (-1, 0, 1)
        for dz in (-1, 0, 1)
        if (dx, dy, dz) != (0, 0, 0)
    ],
    key=lambda d: (-abs(d[2]), abs(d[0]) + abs(d[1])),
)
AXES = ("gx", "gy", "gz")


def span_of(step, side):
    if step == 0:
        return slice(1, 5)
    if side == "source":
        return slice(4, 5) if step > 0 else slice(1, 2)
    return slice(0, 1) if step > 0 else slice(5, 6)


def kernel(
    sizes,
    right_ref,
    bond_ref,
    open_ref,
    onsite_ref,
    level_ref,
    shift_ref,
    sol_ref,
    res_ref,
    ext,
    last,
    diag,
    natural,
    flipped,
    stage1,
    stage2,
    stage3,
    from_x,
    from_y,
    from_z,
    matrix_t,
    matrix_hi,
    matrix_lo,
    sums,
    slots,
    load_sem,
    send_sem,
    recv_sem,
    coef_send,
    coef_recv,
    sum_send,
    sum_recv,
):
    me = [lax.axis_index(name) for name in AXES]

    def at(step):
        return tuple(lax.rem(me[n] + (step[n] + sizes[n]), sizes[n]) for n in range(3))

    def remote(source, target, send, recv, step):
        return pltpu.make_async_remote_copy(
            src_ref=source,
            dst_ref=target,
            send_sem=send,
            recv_sem=recv,
            device_id=at(step),
            device_id_type=pl.DeviceIdType.MESH,
        )

    sum_steps = (
        [(0, 0, n) for n in range(1, sizes[2])],
        [(0, n, 0) for n in range(1, sizes[1])],
        [(n, 0, 0) for n in range(1, sizes[0])],
    )
    peers = {tuple(d[n] % sizes[n] for n in range(3)) for d in directions}
    for steps in sum_steps:
        peers |= set(steps)
    peers = sorted(peers)

    load = pltpu.make_async_copy(right_ref, ext.at[0, 1:5, 1:5, 1:5], load_sem)
    load.start()
    barrier = pltpu.get_barrier_semaphore()
    for step in peers:
        pl.semaphore_signal(
            barrier, inc=1, device_id=at(step), device_id_type=pl.DeviceIdType.MESH
        )

    blocks = bond_ref[...] * open_ref[...].astype(f32)
    table = blocks.reshape(1024, 13).T
    for orb in range(4):
        natural[:, orb, :] = table[:, 256 * orb : 256 * orb + 256]
    table = jnp.swapaxes(blocks, 0, 1).reshape(1024, 13).T
    for orb in range(4):
        flipped[:, orb, :] = table[:, 256 * orb : 256 * orb + 256]

    pl.semaphore_wait(barrier, len(peers))

    waiting = []
    coef_x = remote(natural.at[4:13], from_x, coef_send.at[0], coef_recv.at[0], (1, 0, 0))
    coef_x.start()

    def exchange(number):
        copies = []
        for index, step in enumerate(directions):
            copy = remote(
                ext.at[(number,) + tuple(span_of(s, "source") for s in step)],
                ext.at[(number,) + tuple(span_of(s, "target") for s in step)],
                send_sem.at[number, index],
                recv_sem.at[number, index],
                step,
            )
            copy.start()
            copies.append(copy)
        return copies

    load.wait()
    copies = exchange(0)
    waiting += copies

    lane = lax.broadcasted_iota(jnp.int32, (4, 256), 1)
    place = ((lane >> 4) & 3, (lane >> 2) & 3, lane & 3)

    def moved(inner, outer, axis, step):
        stride = (16, 4, 1)[axis]
        if step > 0:
            mixed = jnp.where(place[axis] == 3, outer, inner)
            return jnp.where(
                place[axis] == 0,
                pltpu.roll(mixed, 256 - 3 * stride, 1),
                pltpu.roll(mixed, stride, 1),
            )
        mixed = jnp.where(place[axis] == 0, outer, inner)
        return jnp.where(
            place[axis] == 3,
            pltpu.roll(mixed, 3 * stride, 1),
            pltpu.roll(mixed, 256 - stride, 1),
        )

    coef_x.wait()
    for k in range(13):
        if k < 4:
            stage1[k] = natural[k]
        else:
            stage1[k] = moved(natural[k], from_x[k - 4], 0, 1)
    coef_y = [
        remote(stage1.at[1:4], from_y.at[0:3], coef_send.at[1], coef_recv.at[1], (0, 1, 0)),
        remote(stage1.at[10:13], from_y.at[3:6], coef_send.at[2], coef_recv.at[2], (0, 1, 0)),
        remote(stage1.at[4:7], from_y.at[6:9], coef_send.at[3], coef_recv.at[3], (0, -1, 0)),
    ]
    for copy in coef_y:
        copy.start()
    for copy in coef_y:
        copy.wait()
    slot_y = {1: 0, 2: 1, 3: 2, 10: 3, 11: 4, 12: 5, 4: 6, 5: 7, 6: 8}
    for k in range(13):
        if k in slot_y:
            stage2[k] = moved(stage1[k], from_y[slot_y[k]], 1, half_offsets[k][1])
        else:
            stage2[k] = stage1[k]
    order_z = [0, 3, 6, 9, 12, 1, 4, 7, 10]
    coef_z = []
    for index, k in enumerate(order_z):
        copy = remote(
            stage2.at[k],
            from_z.at[index],
            coef_send.at[4 + index],
            coef_recv.at[4 + index],
            (0, 0, half_offsets[k][2]),
        )
        copy.start()
        coef_z.append(copy)
    for copy in coef_z:
        copy.wait()
    for k in range(13):
        if k in order_z:
            stage3[k] = moved(stage2[k], from_z[order_z.index(k)], 2, half_offsets[k][2])
        else:
            stage3[k] = stage2[k]

    table = {(0, 0, 0): onsite_ref[...]}
    for k, offset in enumerate(half_offsets):
        table[offset] = flipped[k]
        table[tuple(-o for o in offset)] = stage3[k]
    for axis in range(3):
        kind = place[axis]
        kind = jnp.where(kind == 3, 0, kind)
        fresh = {}
        for key in table:
            cls = key[axis] % 3
            picks = []
            for residue in range(3):
                step = (cls - residue + 1) % 3 - 1
                picks.append(table[key[:axis] + (step,) + key[axis + 1 :]])
            fresh[key] = jnp.where(
                kind == 0, picks[0], jnp.where(kind == 1, picks[1], picks[2])
            )
        table = fresh
    near = [
        [(place[axis] >= e - 1) & (place[axis] <= e + 1) for e in range(-1, 5)]
        for axis in range(3)
    ]
    row = 0
    for ex in range(-1, 5):
        for ey in range(-1, 5):
            both = near[0][ex + 1] & near[1][ey + 1]
            for ez in range(-1, 5):
                key = tuple((e + 1) % 3 - 1 for e in (ex, ey, ez))
                matrix_t[row : row + 4, :] = jnp.where(both & near[2][ez + 1], table[key], 0.0)
                row += 4

    out_row = lax.broadcasted_iota(jnp.int32, (256, 256), 0)
    out_lane = lax.broadcasted_iota(jnp.int32, (256, 256), 1)
    same = ((out_row & 3) == (out_lane >> 6)) & ((out_row >> 2) == (out_lane & 63))
    pick = jnp.where(same, 1.0, 0.0).astype(bf16)
    entries = matrix_t[...]
    high = entries.astype(bf16)
    low = (entries - high.astype(f32)).astype(bf16)
    across = (((1,), (1,)), ((), ()))
    matrix_hi[...] = lax.dot_general(pick, high, across, preferred_element_type=f32).astype(bf16)
    matrix_lo[...] = lax.dot_general(pick, low, across, preferred_element_type=f32).astype(bf16)
    levels = jnp.sum(
        jnp.where(same, level_ref[...] - CENTRE, 0.0), axis=1, keepdims=True
    )
    diag[...] = jnp.broadcast_to(levels, (256, 256)).reshape(4, 4, 4, 4, 256)

    def core(number):
        return ext[number, 1:5, 1:5, 1:5]

    def applied(number):
        for copy in copies:
            copy.wait_recv()
        whole = ext[number].reshape(864, 256)
        high = whole.astype(bf16)
        low = (whole - high.astype(f32)).astype(bf16)
        total = (
            jnp.dot(matrix_hi[...], low, preferred_element_type=f32)
            + jnp.dot(matrix_lo[...], high, preferred_element_type=f32)
            + jnp.dot(matrix_hi[...], high, preferred_element_type=f32)
        )
        return total.reshape(4, 4, 4, 4, 256) + diag[...] * core(number)

    def product(left, right):
        return jnp.sum(jnp.sum(left * right, axis=(0, 1, 2)), axis=0, keepdims=True)

    ext[1, 1:5, 1:5, 1:5] = applied(0)
    copies = exchange(1)
    waiting += copies
    sums[0, 0:1] = product(core(0), core(0))
    sums[0, 1:2] = product(core(0), core(1))
    sums[0, 3:4] = product(core(1), core(1))
    ext[2, 1:5, 1:5, 1:5] = applied(1) - GAMMA1 * core(0)
    copies = exchange(2)
    waiting += copies
    sums[0, 2:3] = product(core(0), core(2))
    sums[0, 4:5] = product(core(1), core(2))
    sums[0, 5:6] = product(core(2), core(2))
    sums[0, 7:8] = jnp.zeros((1, 256), f32)
    last[...] = applied(2) - GAMMA2 * core(1)
    sums[0, 6:7] = product(core(2), last[...])

    base = 0
    for stage, steps in enumerate(sum_steps):
        sent = []
        for index, step in enumerate(steps):
            copy = remote(
                sums.at[stage],
                slots.at[base + index],
                sum_send.at[base + index],
                sum_recv.at[base + index],
                step,
            )
            copy.start()
            sent.append(copy)
        total = sums[stage]
        for index, copy in enumerate(sent):
            copy.wait_recv()
            total = total + slots[base + index]
        sums[stage + 1] = total
        waiting += sent
        base += len(steps)

    g00, g01, g02, g11, g12, g22, g23 = [sums[3, n : n + 1] for n in range(7)]
    theta = shift_ref[...] + CENTRE
    g03 = g12 - GAMMA2 * g01
    g13 = g22 + GAMMA1 * g02 - GAMMA2 * g11
    a0 = g00 / (theta * g00 + g01)
    s0 = a0
    r0, r1 = 1.0 - a0 * theta, -a0
    rr1 = r0 * r0 * g00 + 2.0 * r0 * r1 * g01 + r1 * r1 * g11
    p0, p1 = r0 + rr1 / g00, r1
    q0, q1, q2 = theta * p0 + GAMMA1 * p1, p0 + theta * p1, p1
    pq = p0 * (q0 * g00 + q1 * g01 + q2 * g02) + p1 * (q0 * g01 + q1 * g11 + q2 * g12)
    a1 = rr1 / pq
    s0, s1 = s0 + a1 * p0, a1 * p1
    r0, r1, r2 = r0 - a1 * q0, r1 - a1 * q1, -a1 * q2
    rr2 = (
        r0 * (r0 * g00 + r1 * g01 + r2 * g02)
        + r1 * (r0 * g01 + r1 * g11 + r2 * g12)
        + r2 * (r0 * g02 + r1 * g12 + r2 * g22)
    )
    ratio = rr2 / rr1
    p0, p1, p2 = r0 + ratio * p0, r1 + ratio * p1, r2
    q0 = theta * p0 + GAMMA1 * p1
    q1 = p0 + theta * p1 + GAMMA2 * p2
    q2 = p1 + theta * p2
    q3 = p2
    pq = (
        p0 * (q0 * g00 + q1 * g01 + q2 * g02 + q3 * g03)
        + p1 * (q0 * g01 + q1 * g11 + q2 * g12 + q3 * g13)
        + p2 * (q0 * g02 + q1 * g12 + q2 * g22 + q3 * g23)
    )
    a2 = rr2 / pq
    s0, s1, s2 = s0 + a2 * p0, s1 + a2 * p1, a2 * p2
    r0, r1, r2, r3 = r0 - a2 * q0, r1 - a2 * q1, r2 - a2 * q2, -a2 * q3
    sol_ref[...] = s0 * core(0) + s1 * core(1) + s2 * core(2)
    res_ref[...] = r0 * core(0) + r1 * core(1) + r2 * core(2) + r3 * last[...]
    for copy in waiting:
        copy.wait_send()


def solution(mesh):
    sizes = tuple(mesh.shape[name] for name in AXES)

    def per_device(right_side, bond_blocks, bond_open, onsite_blocks, orbital_levels, column_shift):
        onsite = (0.5 * (onsite_blocks + jnp.swapaxes(onsite_blocks, 0, 1))).reshape(4, 256)
        levels = orbital_levels.reshape(1, 256)
        bonds = jnp.transpose(bond_blocks, (1, 2, 3, 4, 5, 0))
        opened = jnp.transpose(bond_open, (1, 2, 3, 0))
        vmem = pl.BlockSpec(memory_space=pltpu.VMEM)
        shape = jax.ShapeDtypeStruct((4, 4, 4, 4, 256), f32)
        n_sums = sum(sizes) - 3
        return pl.pallas_call(
            functools.partial(kernel, sizes),
            out_shape=(shape, shape),
            in_specs=[pl.BlockSpec(memory_space=pl.ANY)] + [vmem] * 5,
            out_specs=(vmem, vmem),
            scratch_shapes=[
                pltpu.VMEM((3, 6, 6, 6, 4, 256), f32),
                pltpu.VMEM((4, 4, 4, 4, 256), f32),
                pltpu.VMEM((4, 4, 4, 4, 256), f32),
                pltpu.VMEM((13, 4, 256), f32),
                pltpu.VMEM((13, 4, 256), f32),
                pltpu.VMEM((13, 4, 256), f32),
                pltpu.VMEM((13, 4, 256), f32),
                pltpu.VMEM((13, 4, 256), f32),
                pltpu.VMEM((9, 4, 256), f32),
                pltpu.VMEM((9, 4, 256), f32),
                pltpu.VMEM((9, 4, 256), f32),
                pltpu.VMEM((864, 256), f32),
                pltpu.VMEM((256, 864), bf16),
                pltpu.VMEM((256, 864), bf16),
                pltpu.VMEM((4, 8, 256), f32),
                pltpu.VMEM((n_sums, 8, 256), f32),
                pltpu.SemaphoreType.DMA,
                pltpu.SemaphoreType.DMA((3, 26)),
                pltpu.SemaphoreType.DMA((3, 26)),
                pltpu.SemaphoreType.DMA((13,)),
                pltpu.SemaphoreType.DMA((13,)),
                pltpu.SemaphoreType.DMA((n_sums,)),
                pltpu.SemaphoreType.DMA((n_sums,)),
            ],
            compiler_params=pltpu.CompilerParams(collective_id=0, has_side_effects=True),
        )(right_side, bonds, opened, onsite, levels, column_shift.reshape(1, 256))

    return jax.shard_map(
        per_device,
        mesh=mesh,
        in_specs=(
            P("gx", "gy", "gz", None, None),
            P(None, None, None, "gx", "gy", "gz"),
            P(None, "gx", "gy", "gz"),
            P(None, None, "gx", "gy", "gz"),
            P(None, "gx", "gy", "gz"),
            P(),
        ),
        out_specs=(P("gx", "gy", "gz", None, None), P("gx", "gy", "gz", None, None)),
        check_vma=False,
    )
```

time: 353 us -> 59.5 us (0.17)
  the two profiles are of different devices: /device:TPU:0 before, /device:TPU:1 now
where the time goes in v1:
time: 59.5 us; the launch traced here: 59.2 us
  Pallas kernels  53 us (89%)
  local copies, waits for them, and re-layouts  4.61 us (8%)
  other arithmetic  1.02 us (2%)
  between operations  0.65 us (1%)
    pallas_call x1, Pallas kernels, per_device(): pl.pallas_call(functools.partial(kernel, sizes), out_shape=(shape, shape)...  53 us
    unnamed x4, local copies, waits for them, and re-layouts  2.42 us
    reshape x1, local copies, waits for them, and re-layouts, per_device(): levels = orbital_levels.reshape(1, 256)  1.43 us

profile of v1, /device:TPU:1, one launch (start us, length us, event | category | flops | bytes accessed | tf_op | source)
XLA Modules:
  0.0 59.2 jit_solution(7379776880225988320)
XLA Ops:
  0.6 1.4 %reshape.14.level_ref = f32[1,256]{1,0:T(1,128)} reshape(f32[4,4,4,4]{3,2,1,0:T(4,128)} %param.10) | data formatting | bytes 2048 | tf_op jit(solution)/shard_map/reshape | solution.py:350
  2.1 1.0 %fusion = f32[4,4,4,4,4]{4,3,2,1,0:T(4,128)S(1)} fusion(f32[4,4,4,4,4]{4,3,2,1,0:T(4,128)} %param.9), kind=kLoop, calls=%fused_computation.1 | loop fusion | flops 2048 | bytes 8192 | tf_op jit(solution)/shard_map/mul | solution.py:349
  3.1 0.8 %reshape.13.onsite_ref = f32[4,256]{1,0:T(4,128)} reshape(f32[4,4,4,4,4]{4,3,2,1,0:T(4,128)S(1)} %fusion) | data formatting | bytes 8192 | tf_op jit(solution)/shard_map/reshape | solution.py:349
  3.8 53.0 %shard_map.77 = (f32[4,4,4,4,256]{4,3,2,1,0:T(4,128)}, f32[4,4,4,4,256]{4,3,2,1,0:T(4,128)}) custom-call(f32[4,4,4,4,256]{4,3,2,1,0:T(4,128)} %right_ref.1, f32[4,4,4,4,4,13]{5,4,3,2,1,0:T(4,128)} %bitcast.7, s32[4,4,4,13]{3,2,1,0:T(4,128)} %bitcast.8, f32[4,256]{1,0:T(4,128)} %reshape.13.onsite_ref, f32[1,256]{1,0:T(1,128)} %reshape.14.level_ref, ...), custom_call_target="tpu_custom_call" | custom-call | tf_op jit(solution)/shard_map/pallas_call | solution.py:356
  56.8 0.0 copy-start
  56.8 1.7 %copy.12 = f32[4,4,4,4,256]{4,3,2,1,0:T(4,128)} copy(f32[4,4,4,4,256]{4,3,2,1,0:T(4,128)} %get-tuple-element.4) | data formatting | bytes 524288
  58.5 0.0 copy-done
  58.5 0.7 %copy.13 = f32[4,4,4,4,256]{4,3,2,1,0:T(4,128)} copy(f32[4,4,4,4,256]{4,3,2,1,0:T(4,128)S(1)} %copy-done) | data formatting | bytes 524288
Async XLA Ops:
  56.8 1.7 %copy-start = (f32[4,4,4,4,256]{4,3,2,1,0:T(4,128)S(1)}, f32[4,4,4,4,256]{4,3,2,1,0:T(4,128)}, u32[]{:S(2)}) copy-start(f32[4,4,4,4,256]{4,3,2,1,0:T(4,128)} %get-tuple-element.5) | copy-start | bytes 786436

commit v2 on v0

v2 whole, which is shorter than its diff:
```python
import functools

import jax
import jax.numpy as jnp
from jax import lax
from jax.experimental import pallas as pl
from jax.experimental.pallas import tpu as pltpu
from jax.sharding import PartitionSpec as P

f32 = jnp.float32
bf16 = jnp.bfloat16
MESH = pl.DeviceIdType.MESH

CENTRE = 1.95
GAMMA1 = 0.65 * 0.65 / 3.0
GAMMA2 = 0.65 * 0.65 * 4.0 / 15.0
HALVES = 2
WIDTH = 256 // HALVES
AXES = ("gx", "gy", "gz")

ALL = (-1, 0, 1)
every = [(i, j, k) for i in ALL for j in ALL for k in ALL]
half_offsets = [o for o in every if o > (0, 0, 0)]
directions = sorted(
    [o for o in every if o != (0, 0, 0)],
    key=lambda d: (-abs(d[2]), abs(d[0]) + abs(d[1])),
)
hops = sorted(
    {
        tuple(o[n] * keep[n] for n in range(3))
        for o in half_offsets
        for keep in [(i, j, k) for i in (0, 1) for j in (0, 1) for k in (0, 1)]
    }
    - {(0, 0, 0)},
    key=lambda d: (-abs(d[2]), d),
)
cargo = {
    hop: [
        k
        for k, o in enumerate(half_offsets)
        if all(hop[n] in (0, o[n]) for n in range(3))
    ]
    for hop in hops
}
cargo_slot, cargo_start = {}, {}
for hop in hops:
    cargo_start[hop] = len(cargo_slot)
    for k in cargo[hop]:
        cargo_slot[hop, k] = len(cargo_slot)
CARGO = len(cargo_slot)

INSIDE = range(0, 4)
WITH_RIM = range(-1, 5)
groups = [
    (INSIDE, INSIDE, INSIDE),
    ((-1,), WITH_RIM, WITH_RIM),
    ((4,), WITH_RIM, WITH_RIM),
    (INSIDE, (-1,), WITH_RIM),
    (INSIDE, (4,), WITH_RIM),
    (INSIDE, INSIDE, (-1,)),
    (INSIDE, INSIDE, (4,)),
]


def span_of(step, side):
    if step == 0:
        return slice(1, 5)
    if side == "source":
        return slice(4, 5) if step > 0 else slice(1, 2)
    return slice(0, 1) if step > 0 else slice(5, 6)


def reach(values):
    return slice(values[0] + 1, values[-1] + 2)


def split(value):
    high = value.astype(bf16)
    return high, (value - high.astype(f32)).astype(bf16)


def coefficients(g00, g01, g02, g11, g12, g22, g23, theta):
    g03 = g12 - GAMMA2 * g01
    g13 = g22 + GAMMA1 * g02 - GAMMA2 * g11
    a0 = g00 / (theta * g00 + g01)
    s0 = a0
    r0, r1 = 1.0 - a0 * theta, -a0
    rr1 = r0 * r0 * g00 + 2.0 * r0 * r1 * g01 + r1 * r1 * g11
    p0, p1 = r0 + rr1 / g00, r1
    q0, q1, q2 = theta * p0 + GAMMA1 * p1, p0 + theta * p1, p1
    pq = p0 * (q0 * g00 + q1 * g01 + q2 * g02) + p1 * (q0 * g01 + q1 * g11 + q2 * g12)
    a1 = rr1 / pq
    s0, s1 = s0 + a1 * p0, a1 * p1
    r0, r1, r2 = r0 - a1 * q0, r1 - a1 * q1, -a1 * q2
    rr2 = (
        r0 * (r0 * g00 + r1 * g01 + r2 * g02)
        + r1 * (r0 * g01 + r1 * g11 + r2 * g12)
        + r2 * (r0 * g02 + r1 * g12 + r2 * g22)
    )
    ratio = rr2 / rr1
    p0, p1, p2 = r0 + ratio * p0, r1 + ratio * p1, r2
    q0 = theta * p0 + GAMMA1 * p1
    q1 = p0 + theta * p1 + GAMMA2 * p2
    q2 = p1 + theta * p2
    q3 = p2
    pq = (
        p0 * (q0 * g00 + q1 * g01 + q2 * g02 + q3 * g03)
        + p1 * (q0 * g01 + q1 * g11 + q2 * g12 + q3 * g13)
        + p2 * (q0 * g02 + q1 * g12 + q2 * g22 + q3 * g23)
    )
    a2 = rr2 / pq
    return (
        s0 + a2 * p0,
        s1 + a2 * p1,
        a2 * p2,
        r0 - a2 * q0,
        r1 - a2 * q1,
        r2 - a2 * q2,
        -a2 * q3,
    )


def kernel(
    sizes,
    right_ref,
    bond_ref,
    open_ref,
    onsite_ref,
    level_ref,
    shift_ref,
    first_ref,
    second_ref,
    third_ref,
    mix_ref,
    ext,
    last,
    partial,
    diag,
    bonds,
    opened,
    onsite,
    levels,
    natural,
    flipped,
    shifted,
    outgoing,
    incoming,
    matrix_t,
    matrix_hi,
    matrix_lo,
    sums,
    plane_slots,
    line_slots,
    final_sum,
    final_slots,
    load_sem,
    store_sem,
    halo_send,
    halo_recv,
    other_send,
    other_recv,
):
    me = [lax.axis_index(name) for name in AXES]

    def at(step):
        return tuple(lax.rem(me[n] + (step[n] + sizes[n]), sizes[n]) for n in range(3))

    def push(source, target, send, recv, step):
        pltpu.make_async_remote_copy(
            src_ref=source,
            dst_ref=target,
            send_sem=send,
            recv_sem=recv,
            device_id=at(step),
            device_id_type=MESH,
        ).start()

    def settle(like, sem):
        pltpu.make_async_copy(like, like, sem).wait()

    plane = [(i, j, 0) for i in range(sizes[0]) for j in range(sizes[1]) if (i, j) != (0, 0)]
    line = [(0, 0, k) for k in range(1, sizes[2])]
    others = [
        (i, j, k)
        for i in range(sizes[0])
        for j in range(sizes[1])
        for k in range(sizes[2])
        if (i, j, k) != (0, 0, 0)
    ]

    barrier = pltpu.get_barrier_semaphore()
    for step in others:
        pl.semaphore_signal(barrier, inc=1, device_id=at(step), device_id_type=MESH)
    loads = [
        pltpu.make_async_copy(bond_ref, bonds, load_sem.at[0]),
        pltpu.make_async_copy(open_ref, opened, load_sem.at[1]),
        pltpu.make_async_copy(onsite_ref, onsite, load_sem.at[2]),
        pltpu.make_async_copy(level_ref, levels, load_sem.at[3]),
    ]
    for half in range(HALVES):
        loads.append(
            pltpu.make_async_copy(
                right_ref.at[:, :, :, :, half * WIDTH : half * WIDTH + WIDTH],
                ext.at[0, half, 1:5, 1:5, 1:5],
                load_sem.at[4 + half],
            )
        )
    for copy in loads:
        copy.start()

    lane = lax.broadcasted_iota(jnp.int32, (4, 256), 1)
    place = ((lane >> 4) & 3, (lane >> 2) & 3, lane & 3)

    def cyclic(value, axis, step):
        stride = (16, 4, 1)[axis]
        if step == 0:
            return value
        if step > 0:
            return jnp.where(
                place[axis] == 0,
                pltpu.roll(value, 256 - 3 * stride, 1),
                pltpu.roll(value, stride, 1),
            )
        return jnp.where(
            place[axis] == 3,
            pltpu.roll(value, 3 * stride, 1),
            pltpu.roll(value, 256 - stride, 1),
        )

    with jax.named_scope("tables"):
        for copy in loads[:4]:
            copy.wait()
        blocks = bonds[...] * opened[...].astype(f32)
        table = blocks.reshape(1024, 13).T
        for orb in range(4):
            natural[:, orb, :] = table[:, 256 * orb : 256 * orb + 256]
        table = jnp.swapaxes(blocks, 0, 1).reshape(1024, 13).T
        for orb in range(4):
            flipped[:, orb, :] = table[:, 256 * orb : 256 * orb + 256]
        for k, offset in enumerate(half_offsets):
            value = natural[k]
            for axis in range(3):
                value = cyclic(value, axis, offset[axis])
            shifted[k] = value
            for hop in hops:
                if k in cargo[hop]:
                    outgoing[cargo_slot[hop, k]] = value

    with jax.named_scope("w_barrier"):
        pl.semaphore_wait(barrier, len(others))

    for hop in hops:
        rows = slice(cargo_start[hop], cargo_start[hop] + len(cargo[hop]))
        push(outgoing.at[rows], incoming.at[rows], other_send.at[0], other_recv.at[0], hop)

    def exchange(number, half):
        for step in directions:
            push(
                ext.at[(number, half) + tuple(span_of(s, "source") for s in step)],
                ext.at[(number, half) + tuple(span_of(s, "target") for s in step)],
                halo_send.at[number, half],
                halo_recv.at[number, half],
                step,
            )

    def halo_like(number, half):
        return matrix_t.at[0 : 152 * 4 * WIDTH // 256]

    for half in range(HALVES):
        loads[4 + half].wait()
        exchange(0, half)

    out_row = lax.broadcasted_iota(jnp.int32, (256, 256), 0)
    out_lane = lax.broadcasted_iota(jnp.int32, (256, 256), 1)
    same = ((out_row & 3) == (out_lane >> 6)) & ((out_row >> 2) == (out_lane & 63))
    pick = jnp.where(same, 1.0, 0.0).astype(bf16)

    with jax.named_scope("onsite"):
        spread = jnp.where(
            lax.broadcasted_iota(jnp.int32, (4, 256), 0) == (lane & 3), 1.0, 0.0
        )
        raw = onsite[...]
        raw = (0.5 * (raw + jnp.swapaxes(raw, 0, 1))).reshape(256, 4)
        wide = jnp.dot(
            raw, spread, precision=lax.Precision.HIGHEST, preferred_element_type=f32
        )
        keep = ((out_row >> 6) == (out_lane >> 6)) & (
            (out_row & 15) == ((out_lane >> 2) & 15)
        )
        wide = jnp.where(keep, wide, 0.0).reshape(4, 4, 16, 256)
        local = jnp.sum(jnp.sum(wide, axis=0), axis=1)
        wide = jnp.dot(
            levels[...].reshape(64, 4) - CENTRE,
            spread,
            precision=lax.Precision.HIGHEST,
            preferred_element_type=f32,
        )
        keep = out_row[0:64] == (out_lane[0:64] >> 2)
        level = jnp.sum(jnp.where(keep, wide, 0.0), axis=0, keepdims=True)
        level = jnp.sum(jnp.where(same, level, 0.0), axis=1, keepdims=True)
        diag[...] = jnp.broadcast_to(level, (256, WIDTH)).reshape(4, 4, 4, 4, WIDTH)

    near = [
        [(place[axis] >= e - 1) & (place[axis] <= e + 1) for e in WITH_RIM]
        for axis in range(3)
    ]

    def build(chosen, first_row, rows, behind):
        table = {(0, 0, 0): local}
        for k, offset in enumerate(half_offsets):
            table[offset] = flipped[k]
            table[tuple(-o for o in offset)] = behind(k, offset)
        for axis in range(3):
            kind = jnp.where(place[axis] == 3, 0, place[axis])
            fresh = {}
            for key in table:
                picks = []
                for residue in range(3):
                    step = (key[axis] % 3 - residue + 1) % 3 - 1
                    picks.append(table[key[:axis] + (step,) + key[axis + 1 :]])
                fresh[key] = jnp.where(
                    kind == 0, picks[0], jnp.where(kind == 1, picks[1], picks[2])
                )
            table = fresh
        row = first_row
        for group in chosen:
            for ex in group[0]:
                for ey in group[1]:
                    both = near[0][ex + 1] & near[1][ey + 1]
                    for ez in group[2]:
                        key = tuple((e + 1) % 3 - 1 for e in (ex, ey, ez))
                        matrix_t[row : row + 4, :] = jnp.where(
                            both & near[2][ez + 1], table[key], 0.0
                        )
                        row += 4
        across = (((1,), (1,)), ((), ()))
        span = slice(first_row, first_row + rows)
        high, low = split(matrix_t[span, :])
        matrix_hi[:, span] = lax.dot_general(
            pick, high, across, preferred_element_type=f32
        ).astype(bf16)
        matrix_lo[:, span] = lax.dot_general(
            pick, low, across, preferred_element_type=f32
        ).astype(bf16)

    def mirrored(k, offset):
        axes = [n for n in range(3) if offset[n]]

        def choose(position, hop):
            if position == len(axes):
                return incoming[cargo_slot[hop, k]] if any(hop) else shifted[k]
            axis = axes[position]
            edge = 0 if offset[axis] > 0 else 3
            away = hop[:axis] + (offset[axis],) + hop[axis + 1 :]
            return jnp.where(
                place[axis] == edge, choose(position + 1, away), choose(position + 1, hop)
            )

        return choose(0, (0, 0, 0))

    def times(span, value):
        high, low = split(value)
        return (
            jnp.dot(matrix_hi[:, span], low, preferred_element_type=f32)
            + jnp.dot(matrix_lo[:, span], high, preferred_element_type=f32)
            + jnp.dot(matrix_hi[:, span], high, preferred_element_type=f32)
        )

    def core(number, half):
        return ext[number, half, 1:5, 1:5, 1:5]

    def before(number, half):
        partial[half] = times(slice(0, 256), core(number, half).reshape(256, WIDTH))

    def after(number, half):
        with jax.named_scope("w_halo%d" % (2 * number + half)):
            settle(halo_like(number, half), halo_recv.at[number, half])
        rim = jnp.concatenate(
            [
                ext[(number, half) + tuple(reach(v) for v in group)].reshape(-1, WIDTH)
                for group in groups[1:]
            ],
            axis=0,
        )
        total = partial[half] + times(slice(256, 864), rim)
        return total.reshape(4, 4, 4, 4, WIDTH) + diag[...] * core(number, half)

    def product(left, right):
        return jnp.sum(jnp.sum(left * right, axis=(0, 1, 2)), axis=0, keepdims=True)

    stores = []

    def keep_copy(source, target, number, half):
        copy = pltpu.make_async_copy(
            source,
            target.at[:, :, :, :, half * WIDTH : half * WIDTH + WIDTH],
            store_sem.at[number, half],
        )
        copy.start()
        stores.append(copy)

    with jax.named_scope("inner"):
        build(groups[:1], 0, 256, lambda k, offset: shifted[k])
        for half in range(HALVES):
            before(0, half)
    with jax.named_scope("w_coef"):
        settle(incoming, other_recv.at[0])
    with jax.named_scope("rim"):
        build(groups[1:], 256, 608, mirrored)

    def lanes(half):
        return slice(half * WIDTH, half * WIDTH + WIDTH)

    for half in range(HALVES):
        ext[1, half, 1:5, 1:5, 1:5] = after(0, half)
        exchange(1, half)
        keep_copy(ext.at[1, half, 1:5, 1:5, 1:5], first_ref, 0, half)
        before(1, half)
        sums[0, 0, :, lanes(half)] = product(core(0, half), core(0, half))
        sums[0, 1, :, lanes(half)] = product(core(0, half), core(1, half))
        sums[0, 3, :, lanes(half)] = product(core(1, half), core(1, half))
    for half in range(HALVES):
        ext[2, half, 1:5, 1:5, 1:5] = after(1, half) - GAMMA1 * core(0, half)
        exchange(2, half)
        keep_copy(ext.at[2, half, 1:5, 1:5, 1:5], second_ref, 1, half)
        sums[0, 2, :, lanes(half)] = product(core(0, half), core(2, half))
        sums[0, 4, :, lanes(half)] = product(core(1, half), core(2, half))
        sums[0, 5, :, lanes(half)] = product(core(2, half), core(2, half))
    for index, step in enumerate(plane):
        push(sums.at[0], plane_slots.at[index], other_send.at[1], other_recv.at[1], step)
    for half in range(HALVES):
        before(2, half)
    with jax.named_scope("w_plane"):
        settle(plane_slots, other_recv.at[1])
    sums[1] = sums[0] + jnp.sum(plane_slots[...], axis=0)
    for index, step in enumerate(line):
        push(sums.at[1], line_slots.at[index], other_send.at[2], other_recv.at[2], step)
    for half in range(HALVES):
        last[half] = after(2, half) - GAMMA2 * core(1, half)
        final_sum[:, lanes(half)] = product(core(2, half), last[half])
        keep_copy(last.at[half], third_ref, 2, half)
    for index, step in enumerate(others):
        push(final_sum, final_slots.at[index], other_send.at[3], other_recv.at[3], step)
    with jax.named_scope("w_line"):
        settle(line_slots, other_recv.at[2])
    early = sums[1] + jnp.sum(line_slots[...], axis=0)
    with jax.named_scope("w_stores"):
        for copy in stores:
            copy.wait()
        for number in range(3):
            for half in range(HALVES):
                settle(halo_like(number, half), halo_send.at[number, half])
        settle(outgoing, other_send.at[0])
        settle(plane_slots, other_send.at[1])
        settle(line_slots, other_send.at[2])
    with jax.named_scope("w_final"):
        settle(final_slots, other_recv.at[3])
    g23 = final_sum[...] + jnp.sum(final_slots[...], axis=0)
    mix = coefficients(*[early[n] for n in range(6)], g23, shift_ref[...] + CENTRE)
    for n in range(7):
        mix_ref[n : n + 1, :] = mix[n]
    mix_ref[7:8, :] = jnp.zeros((1, 256), f32)
    settle(final_slots, other_send.at[3])


def solution(mesh):
    sizes = tuple(mesh.shape[name] for name in AXES)
    count = sizes[0] * sizes[1] * sizes[2]

    def per_device(right_side, bond_blocks, bond_open, onsite_blocks, orbital_levels, column_shift):
        vmem = pl.BlockSpec(memory_space=pltpu.VMEM)
        hbm = pl.BlockSpec(memory_space=pl.ANY)
        field = jax.ShapeDtypeStruct((4, 4, 4, 4, 256), f32)
        first, second, third, mix = pl.pallas_call(
            functools.partial(kernel, sizes),
            out_shape=(field, field, field, jax.ShapeDtypeStruct((8, 256), f32)),
            in_specs=[hbm] * 5 + [vmem],
            out_specs=(hbm, hbm, hbm, vmem),
            scratch_shapes=[
                pltpu.VMEM((3, HALVES, 6, 6, 6, 4, WIDTH), f32),
                pltpu.VMEM((HALVES, 4, 4, 4, 4, WIDTH), f32),
                pltpu.VMEM((HALVES, 256, WIDTH), f32),
                pltpu.VMEM((4, 4, 4, 4, WIDTH), f32),
                pltpu.VMEM((4, 4, 4, 4, 4, 13), f32),
                pltpu.VMEM((4, 4, 4, 13), jnp.int32),
                pltpu.VMEM((4, 4, 4, 4, 4), f32),
                pltpu.VMEM((4, 4, 4, 4), f32),
                pltpu.VMEM((13, 4, 256), f32),
                pltpu.VMEM((13, 4, 256), f32),
                pltpu.VMEM((13, 4, 256), f32),
                pltpu.VMEM((CARGO, 4, 256), f32),
                pltpu.VMEM((CARGO, 4, 256), f32),
                pltpu.VMEM((864, 256), f32),
                pltpu.VMEM((256, 864), bf16),
                pltpu.VMEM((256, 864), bf16),
                pltpu.VMEM((2, 6, 1, 256), f32),
                pltpu.VMEM((sizes[0] * sizes[1] - 1, 6, 1, 256), f32),
                pltpu.VMEM((sizes[2] - 1, 6, 1, 256), f32),
                pltpu.VMEM((1, 256), f32),
                pltpu.VMEM((count - 1, 1, 256), f32),
                pltpu.SemaphoreType.DMA((4 + HALVES,)),
                pltpu.SemaphoreType.DMA((3, HALVES)),
                pltpu.SemaphoreType.DMA((3, HALVES)),
                pltpu.SemaphoreType.DMA((3, HALVES)),
                pltpu.SemaphoreType.DMA((4,)),
                pltpu.SemaphoreType.DMA((4,)),
            ],
            compiler_params=pltpu.CompilerParams(collective_id=0, has_side_effects=True),
        )(
            right_side,
            jnp.transpose(bond_blocks, (1, 2, 3, 4, 5, 0)),
            jnp.transpose(bond_open, (1, 2, 3, 0)),
            onsite_blocks,
            orbital_levels,
            column_shift.reshape(1, 256),
        )
        answer = mix[0] * right_side + mix[1] * first + mix[2] * second
        left = mix[3] * right_side + mix[4] * first + mix[5] * second + mix[6] * third
        return answer, left

    return jax.shard_map(
        per_device,
        mesh=mesh,
        in_specs=(
            P("gx", "gy", "gz", None, None),
            P(None, None, None, "gx", "gy", "gz"),
            P(None, "gx", "gy", "gz"),
            P(None, None, "gx", "gy", "gz"),
            P(None, "gx", "gy", "gz"),
            P(),
        ),
        out_specs=(P("gx", "gy", "gz", None, None), P("gx", "gy", "gz", None, None)),
        check_vma=False,
    )
```

time: 353 us -> 46.4 us (0.13)
  the two profiles are of different devices: /device:TPU:0 before, /device:TPU:1 now
where the time goes in v2:
time: 46.4 us; the launch traced here: 46.2 us
  Pallas kernels  42.4 us (91%)
  other arithmetic  2.14 us (5%)
  local copies, waits for them, and re-layouts  0.97 us (2%)
  between operations  0.65 us (1%)
    pallas_call x1, Pallas kernels, per_device(): pl.pallas_call(functools.partial(kernel, sizes), out_shape=(field, field,...  42.4 us
    add x1, other arithmetic, per_device(): mix[3] * right_side + mix[4] * first + mix[5] * second + mix[6] * third  2.14 us
    slice x1, local copies, waits for them, and re-layouts, per_device(): mix[3] * right_side + mix[4] * first + mix[5] * second + mix[6] * third  0.96 us

profile of v2, /device:TPU:1, one launch (start us, length us, event | category | flops | bytes accessed | tf_op | source)
XLA Modules:
  0.0 46.2 jit_solution(9954246796652397597)
XLA Ops:
  0.6 0.0 copy-start
  0.6 42.4 %shard_map.77 = (f32[4,4,4,4,256]{4,3,2,1,0:T(4,128)}, f32[4,4,4,4,256]{4,3,2,1,0:T(4,128)}, f32[4,4,4,4,256]{4,3,2,1,0:T(4,128)}, f32[8,256]{1,0:T(8,128)}) custom-call(f32[4,4,4,4,256]{4,3,2,1,0:T(4,128)} %right_ref.1, f32[4,4,4,4,4,13]{5,4,3,2,1,0:T(4,128)} %bitcast.10, s32[4,4,4,13]{3,2,1,0:T(4,128)} %bitcast.11, f32[4,4,4,4,4]{4,3,2,1,0:T(4,128)} %onsite_ref.1, ...), custom_call_target="tpu_custom_call" | custom-call | tf_op jit(solution)/shard_map/pallas_call | solution.py:474
  43.1 1.0 %fusion = (f32[1,256]{1,0:T(1,128)S(1)}, f32[1,256]{1,0:T(1,128)S(1)}, f32[1,256]{1,0:T(1,128)S(1)}, f32[1,256]{1,0:T(1,128)S(1)}, f32[1,256]{1,0:T(1,128)S(1)}, /*index=5*/f32[1,256]{1,0:T(1,128)S(1)}, f32[1,256]{1,0:T(1,128)S(1)}) fusion(f32[8,256]{1,0:T(8,128)} %get-tuple-element.6), kind=kLoop, calls=%fused_computation.2 | loop fusion | bytes 14336 | tf_op jit(solution)/shard_map/slice | solution.py:518
  44.0 0.0 copy-done
  44.0 2.1 %multiply_add_fusion = (f32[4,4,4,4,256]{4,3,2,1,0:T(4,128)}, f32[4,4,4,4,256]{4,3,2,1,0:T(4,128)}) fusion(f32[4,4,4,4,256]{4,3,2,1,0:T(4,128)} %get-tuple-element.9, f32[4,4,4,4,256]{4,3,2,1,0:T(4,128)} %get-tuple-element.8, f32[4,4,4,4,256]{4,3,2,1,0:T(4,128)} %get-tuple-element.7, f32[4,4,4,4,256]{4,3,2,1,0:T(4,128)S(1)} %copy-done, f32[256]{0:T(256)S(1)} %bitcast.13, ...), kind=kLoop, calls=%fused_computation | loop fusion | flops 786432 | bytes 1580032 | tf_op jit(solution)/shard_map/add | solution.py:518
Async XLA Ops:
  0.6 43.4 %copy-start = (f32[4,4,4,4,256]{4,3,2,1,0:T(4,128)S(1)}, f32[4,4,4,4,256]{4,3,2,1,0:T(4,128)}, u32[]{:S(2)}) copy-start(f32[4,4,4,4,256]{4,3,2,1,0:T(4,128)} %right_ref.1) | copy-start | bytes 786436

commit v3 on v2

--- a/solution.py
+++ b/solution.py
@@ -42,23 +42,27 @@
     ]
     for hop in hops
 }
-cargo_slot, cargo_start = {}, {}
+cargo_slot, slabs = {}, []
+cargo_start = {}
 for hop in hops:
-    cargo_start[hop] = len(cargo_slot)
-    for k in cargo[hop]:
-        cargo_slot[hop, k] = len(cargo_slot)
-CARGO = len(cargo_slot)
+    cargo_start[hop] = len(slabs)
+    for index, k in enumerate(cargo[hop]):
+        if index % 4 == 0:
+            slabs.append((hop, []))
+        slabs[-1][1].append(k)
+        cargo_slot[hop, k] = (len(slabs) - 1, index % 4)
+CARGO = len(slabs)
 
 INSIDE = range(0, 4)
 WITH_RIM = range(-1, 5)
 groups = [
     (INSIDE, INSIDE, INSIDE),
-    ((-1,), WITH_RIM, WITH_RIM),
-    ((4,), WITH_RIM, WITH_RIM),
-    (INSIDE, (-1,), WITH_RIM),
-    (INSIDE, (4,), WITH_RIM),
-    (INSIDE, INSIDE, (-1,)),
-    (INSIDE, INSIDE, (4,)),
+    ((4,), WITH_RIM, INSIDE),
+    ((-1,), WITH_RIM, INSIDE),
+    (INSIDE, (-1,), INSIDE),
+    (INSIDE, (4,), INSIDE),
+    (WITH_RIM, WITH_RIM, (-1,)),
+    (WITH_RIM, WITH_RIM, (4,)),
 ]
 
 
@@ -79,7 +83,7 @@
     return high, (value - high.astype(f32)).astype(bf16)
 
 
-def coefficients(g00, g01, g02, g11, g12, g22, g23, theta):
+def early_part(g00, g01, g02, g11, g12, g22, theta):
     g03 = g12 - GAMMA2 * g01
     g13 = g22 + GAMMA1 * g02 - GAMMA2 * g11
     a0 = g00 / (theta * g00 + g01)
@@ -106,18 +110,9 @@
     pq = (
         p0 * (q0 * g00 + q1 * g01 + q2 * g02 + q3 * g03)
         + p1 * (q0 * g01 + q1 * g11 + q2 * g12 + q3 * g13)
-        + p2 * (q0 * g02 + q1 * g12 + q2 * g22 + q3 * g23)
+        + p2 * (q0 * g02 + q1 * g12 + q2 * g22)
     )
-    a2 = rr2 / pq
-    return (
-        s0 + a2 * p0,
-        s1 + a2 * p1,
-        a2 * p2,
-        r0 - a2 * q0,
-        r1 - a2 * q1,
-        r2 - a2 * q2,
-        -a2 * q3,
-    )
+    return rr2, pq, p2 * q3, (s0, s1, 0.0, r0, r1, r2, 0.0), (p0, p1, p2, -q0, -q1, -q2, -q3)
 
 
 def kernel(
@@ -128,6 +123,7 @@
     onsite_ref,
     level_ref,
     shift_ref,
+    zeroth_ref,
     first_ref,
     second_ref,
     third_ref,
@@ -148,6 +144,9 @@
     matrix_t,
     matrix_hi,
     matrix_lo,
+    first_sum,
+    first_plane,
+    first_line,
     sums,
     plane_slots,
     line_slots,
@@ -159,6 +158,8 @@
     halo_recv,
     other_send,
     other_recv,
+    final_send,
+    final_recv,
 ):
     me = [lax.axis_index(name) for name in AXES]
 
@@ -188,25 +189,30 @@
         if (i, j, k) != (0, 0, 0)
     ]
 
-    barrier = pltpu.get_barrier_semaphore()
-    for step in others:
-        pl.semaphore_signal(barrier, inc=1, device_id=at(step), device_id_type=MESH)
-    loads = [
-        pltpu.make_async_copy(bond_ref, bonds, load_sem.at[0]),
-        pltpu.make_async_copy(open_ref, opened, load_sem.at[1]),
-        pltpu.make_async_copy(onsite_ref, onsite, load_sem.at[2]),
-        pltpu.make_async_copy(level_ref, levels, load_sem.at[3]),
-    ]
+    greeted = {tuple(d[n] % sizes[n] for n in range(3)) for d in directions}
+    greeted = sorted(greeted | set(plane) | set(line))
+
+    loads = []
     for half in range(HALVES):
         loads.append(
             pltpu.make_async_copy(
                 right_ref.at[:, :, :, :, half * WIDTH : half * WIDTH + WIDTH],
                 ext.at[0, half, 1:5, 1:5, 1:5],
-                load_sem.at[4 + half],
+                load_sem.at[half],
             )
         )
-    for copy in loads:
+    tables = [
+        pltpu.make_async_copy(bond_ref, bonds, load_sem.at[HALVES]),
+        pltpu.make_async_copy(open_ref, opened, load_sem.at[HALVES + 1]),
+        pltpu.make_async_copy(onsite_ref, onsite, load_sem.at[HALVES + 2]),
+        pltpu.make_async_copy(level_ref, levels, load_sem.at[HALVES + 3]),
+    ]
+    for copy in tables + loads:
         copy.start()
+    barrier = pltpu.get_barrier_semaphore()
+    with jax.named_scope("greet"):
+        for step in greeted:
+            pl.semaphore_signal(barrier, inc=1, device_id=at(step), device_id_type=MESH)
 
     lane = lax.broadcasted_iota(jnp.int32, (4, 256), 1)
     place = ((lane >> 4) & 3, (lane >> 2) & 3, lane & 3)
@@ -227,8 +233,28 @@
             pltpu.roll(value, 256 - stride, 1),
         )
 
+    def layer(hop):
+        axis = [n for n in range(3) if hop[n]][0]
+        return axis, (16, 4, 1)[axis], 0 if hop[axis] > 0 else 3
+
+    def packed(hop, values):
+        axis, stride, edge = layer(hop)
+        total = values[0]
+        for index in range(1, len(values)):
+            spot = (edge + index) % 4
+            moved = pltpu.roll(values[index], (stride * (spot - edge)) % 256, 1)
+            total = jnp.where(place[axis] == spot, moved, total)
+        return total
+
+    def unpacked(hop, k):
+        axis, stride, edge = layer(hop)
+        slot, index = cargo_slot[hop, k]
+        spot = (edge + index) % 4
+        value = incoming[slot]
+        return value if index == 0 else pltpu.roll(value, (stride * (edge - spot)) % 256, 1)
+
     with jax.named_scope("tables"):
-        for copy in loads[:4]:
+        for copy in tables:
             copy.wait()
         blocks = bonds[...] * opened[...].astype(f32)
         table = blocks.reshape(1024, 13).T
@@ -242,32 +268,31 @@
             for axis in range(3):
                 value = cyclic(value, axis, offset[axis])
             shifted[k] = value
-            for hop in hops:
-                if k in cargo[hop]:
-                    outgoing[cargo_slot[hop, k]] = value
-
-    with jax.named_scope("w_barrier"):
-        pl.semaphore_wait(barrier, len(others))
-
-    for hop in hops:
-        rows = slice(cargo_start[hop], cargo_start[hop] + len(cargo[hop]))
-        push(outgoing.at[rows], incoming.at[rows], other_send.at[0], other_recv.at[0], hop)
+        for slot, (hop, blocks) in enumerate(slabs):
+            outgoing[slot] = packed(hop, [shifted[k] for k in blocks])
 
     def exchange(number, half):
         for step in directions:
+            part = 1 if step[2] else 0
             push(
                 ext.at[(number, half) + tuple(span_of(s, "source") for s in step)],
                 ext.at[(number, half) + tuple(span_of(s, "target") for s in step)],
                 halo_send.at[number, half],
-                halo_recv.at[number, half],
+                halo_recv.at[number, half, part],
                 step,
             )
 
-    def halo_like(number, half):
-        return matrix_t.at[0 : 152 * 4 * WIDTH // 256]
-
-    for half in range(HALVES):
-        loads[4 + half].wait()
+    def halo_like(part):
+        return matrix_t.at[0 : (80, 72, 152)[part] * 4 * WIDTH // 256]
+
+    with jax.named_scope("w_barrier"):
+        pl.semaphore_wait(barrier, len(greeted))
+    for hop in hops:
+        count = sum(1 for slab in slabs if slab[0] == hop)
+        rows = slice(cargo_start[hop], cargo_start[hop] + count)
+        push(outgoing.at[rows], incoming.at[rows], other_send.at[0], other_recv.at[0], hop)
+    for half in range(HALVES):
+        loads[half].wait()
         exchange(0, half)
 
     out_row = lax.broadcasted_iota(jnp.int32, (256, 256), 0)
@@ -348,7 +373,7 @@
 
         def choose(position, hop):
             if position == len(axes):
-                return incoming[cargo_slot[hop, k]] if any(hop) else shifted[k]
+                return unpacked(hop, k) if any(hop) else shifted[k]
             axis = axes[position]
             edge = 0 if offset[axis] > 0 else 3
             away = hop[:axis] + (offset[axis],) + hop[axis + 1 :]
@@ -372,18 +397,24 @@
     def before(number, half):
         partial[half] = times(slice(0, 256), core(number, half).reshape(256, WIDTH))
 
-    def after(number, half):
-        with jax.named_scope("w_halo%d" % (2 * number + half)):
-            settle(halo_like(number, half), halo_recv.at[number, half])
+    def rim_times(number, half, part):
+        with jax.named_scope("w_halo%d_%d" % (2 * number + half, part)):
+            settle(halo_like(part), halo_recv.at[number, half, part])
         rim = jnp.concatenate(
             [
                 ext[(number, half) + tuple(reach(v) for v in group)].reshape(-1, WIDTH)
-                for group in groups[1:]
+                for group in (groups[1:5], groups[5:7])[part]
             ],
             axis=0,
         )
-        total = partial[half] + times(slice(256, 864), rim)
-        return total.reshape(4, 4, 4, 4, WIDTH) + diag[...] * core(number, half)
+        return times((slice(256, 576), slice(576, 864))[part], rim)
+
+    def after(number, half):
+        partial[half] = (partial[half] + rim_times(number, half, 0)) + (
+            diag[...] * core(number, half)
+        ).reshape(256, WIDTH)
+        total = partial[half] + rim_times(number, half, 1)
+        return total.reshape(4, 4, 4, 4, WIDTH)
 
     def product(left, right):
         return jnp.sum(jnp.sum(left * right, axis=(0, 1, 2)), axis=0, keepdims=True)
@@ -399,68 +430,130 @@
         copy.start()
         stores.append(copy)
 
+    def lanes(half):
+        return slice(half * WIDTH, half * WIDTH + WIDTH)
+
+    own = (first_sum, sums)
+    from_plane = (first_plane, plane_slots)
+    along_line = (first_line, line_slots)
+
+    def to_plane(group):
+        for index, step in enumerate(plane):
+            push(
+                own[group].at[0],
+                from_plane[group].at[index],
+                other_send.at[1 + group],
+                other_recv.at[1 + group],
+                step,
+            )
+
+    def to_line(group):
+        with jax.named_scope("w_plane%d" % group):
+            settle(from_plane[group], other_recv.at[1 + group])
+        own[group][1] = own[group][0] + jnp.sum(from_plane[group][...], axis=0)
+        for index, step in enumerate(line):
+            push(
+                own[group].at[1],
+                along_line[group].at[index],
+                other_send.at[3 + group],
+                other_recv.at[3 + group],
+                step,
+            )
+
+    def from_line(group):
+        with jax.named_scope("w_line%d" % group):
+            settle(along_line[group], other_recv.at[3 + group])
+        return own[group][1] + jnp.sum(along_line[group][...], axis=0)
+
+    for half in range(HALVES):
+        keep_copy(ext.at[0, half, 1:5, 1:5, 1:5], zeroth_ref, 0, half)
     with jax.named_scope("inner"):
-        build(groups[:1], 0, 256, lambda k, offset: shifted[k])
+        build(groups[:2], 0, 352, lambda k, offset: shifted[k])
         for half in range(HALVES):
             before(0, half)
+    for half in range(HALVES):
+        first_sum[0, :, :, lanes(half)] = product(core(0, half), core(0, half))[None]
+    to_plane(0)
     with jax.named_scope("w_coef"):
         settle(incoming, other_recv.at[0])
     with jax.named_scope("rim"):
-        build(groups[1:], 256, 608, mirrored)
-
-    def lanes(half):
-        return slice(half * WIDTH, half * WIDTH + WIDTH)
+        build(groups[2:], 352, 512, mirrored)
 
     for half in range(HALVES):
         ext[1, half, 1:5, 1:5, 1:5] = after(0, half)
         exchange(1, half)
-        keep_copy(ext.at[1, half, 1:5, 1:5, 1:5], first_ref, 0, half)
+        keep_copy(ext.at[1, half, 1:5, 1:5, 1:5], first_ref, 1, half)
         before(1, half)
-        sums[0, 0, :, lanes(half)] = product(core(0, half), core(0, half))
-        sums[0, 1, :, lanes(half)] = product(core(0, half), core(1, half))
-        sums[0, 3, :, lanes(half)] = product(core(1, half), core(1, half))
+        if half == 0:
+            to_line(0)
+        sums[0, 0, :, lanes(half)] = product(core(0, half), core(1, half))
+        sums[0, 1, :, lanes(half)] = product(core(1, half), core(1, half))
     for half in range(HALVES):
         ext[2, half, 1:5, 1:5, 1:5] = after(1, half) - GAMMA1 * core(0, half)
         exchange(2, half)
-        keep_copy(ext.at[2, half, 1:5, 1:5, 1:5], second_ref, 1, half)
+        keep_copy(ext.at[2, half, 1:5, 1:5, 1:5], second_ref, 2, half)
+        before(2, half)
         sums[0, 2, :, lanes(half)] = product(core(0, half), core(2, half))
-        sums[0, 4, :, lanes(half)] = product(core(1, half), core(2, half))
-        sums[0, 5, :, lanes(half)] = product(core(2, half), core(2, half))
-    for index, step in enumerate(plane):
-        push(sums.at[0], plane_slots.at[index], other_send.at[1], other_recv.at[1], step)
-    for half in range(HALVES):
-        before(2, half)
-    with jax.named_scope("w_plane"):
-        settle(plane_slots, other_recv.at[1])
-    sums[1] = sums[0] + jnp.sum(plane_slots[...], axis=0)
-    for index, step in enumerate(line):
-        push(sums.at[1], line_slots.at[index], other_send.at[2], other_recv.at[2], step)
+        sums[0, 3, :, lanes(half)] = product(core(1, half), core(2, half))
+        sums[0, 4, :, lanes(half)] = product(core(2, half), core(2, half))
+    to_plane(1)
+    g00 = from_line(0)[0]
     for half in range(HALVES):
         last[half] = after(2, half) - GAMMA2 * core(1, half)
-        final_sum[:, lanes(half)] = product(core(2, half), last[half])
-        keep_copy(last.at[half], third_ref, 2, half)
-    for index, step in enumerate(others):
-        push(final_sum, final_slots.at[index], other_send.at[3], other_recv.at[3], step)
-    with jax.named_scope("w_line"):
-        settle(line_slots, other_recv.at[2])
-    early = sums[1] + jnp.sum(line_slots[...], axis=0)
+        final_sum[half] = product(core(2, half), last[half])
+        for index, step in enumerate(others):
+            push(
+                final_sum.at[half],
+                final_slots.at[half, index],
+                final_send.at[half],
+                final_recv.at[half],
+                step,
+            )
+        keep_copy(last.at[half], third_ref, 3, half)
+    to_line(1)
+    rest = from_line(1)
+    rr2, pq, weight, start, along = early_part(
+        g00, rest[0], rest[2], rest[1], rest[3], rest[4], shift_ref[...] + CENTRE
+    )
     with jax.named_scope("w_stores"):
         for copy in stores:
             copy.wait()
         for number in range(3):
             for half in range(HALVES):
-                settle(halo_like(number, half), halo_send.at[number, half])
+                settle(halo_like(2), halo_send.at[number, half])
         settle(outgoing, other_send.at[0])
-        settle(plane_slots, other_send.at[1])
-        settle(line_slots, other_send.at[2])
-    with jax.named_scope("w_final"):
-        settle(final_slots, other_recv.at[3])
-    g23 = final_sum[...] + jnp.sum(final_slots[...], axis=0)
-    mix = coefficients(*[early[n] for n in range(6)], g23, shift_ref[...] + CENTRE)
+        for group in range(2):
+            settle(from_plane[group], other_send.at[1 + group])
+            settle(along_line[group], other_send.at[3 + group])
+    totals = []
+    for half in range(HALVES):
+        with jax.named_scope("w_final%d" % half):
+            settle(final_slots.at[half], final_recv.at[half])
+        totals.append(final_sum[half] + jnp.sum(final_slots[half], axis=0))
+    a2 = rr2 / (pq + weight * jnp.concatenate(totals, axis=1))
     for n in range(7):
-        mix_ref[n : n + 1, :] = mix[n]
-    mix_ref[7:8, :] = jnp.zeros((1, 256), f32)
-    settle(final_slots, other_send.at[3])
+        mix_ref[n : n + 1, :] = start[n] + a2 * along[n]
+    for half in range(HALVES):
+        settle(final_slots.at[half], final_send.at[half])
+
+
+def combine(zeroth_ref, first_ref, second_ref, third_ref, mix_ref, sol_ref, res_ref, sol, res, sem):
+    copies = []
+    for x in range(4):
+        zeroth, first, second = zeroth_ref[x], first_ref[x], second_ref[x]
+        sol[x] = mix_ref[0] * zeroth + mix_ref[1] * first + mix_ref[2] * second
+        res[x] = (
+            mix_ref[3] * zeroth
+            + mix_ref[4] * first
+            + mix_ref[5] * second
+            + mix_ref[6] * third_ref[x]
+        )
+        copies.append(pltpu.make_async_copy(sol.at[x], sol_ref.at[x], sem.at[0, x]))
+        copies.append(pltpu.make_async_copy(res.at[x], res_ref.at[x], sem.at[1, x]))
+        for copy in copies[-2:]:
+            copy.start()
+    for copy in copies:
+        copy.wait()
 
 
 def solution(mesh):
@@ -470,12 +563,13 @@
     def per_device(right_side, bond_blocks, bond_open, onsite_blocks, orbital_levels, column_shift):
         vmem = pl.BlockSpec(memory_space=pltpu.VMEM)
         hbm = pl.BlockSpec(memory_space=pl.ANY)
-        field = jax.ShapeDtypeStruct((4, 4, 4, 4, 256), f32)
-        first, second, third, mix = pl.pallas_call(
+        out = jax.ShapeDtypeStruct((4, 4, 4, 4, 256), f32)
+        field = pltpu.VMEM((4, 4, 4, 4, 256), f32)
+        kept = pl.pallas_call(
             functools.partial(kernel, sizes),
-            out_shape=(field, field, field, jax.ShapeDtypeStruct((8, 256), f32)),
+            out_shape=(field,) * 4 + (pltpu.VMEM((7, 256), f32),),
             in_specs=[hbm] * 5 + [vmem],
-            out_specs=(hbm, hbm, hbm, vmem),
+            out_specs=(hbm,) * 4 + (vmem,),
             scratch_shapes=[
                 pltpu.VMEM((3, HALVES, 6, 6, 6, 4, WIDTH), f32),
                 pltpu.VMEM((HALVES, 4, 4, 4, 4, WIDTH), f32),
@@ -493,17 +587,22 @@
                 pltpu.VMEM((864, 256), f32),
                 pltpu.VMEM((256, 864), bf16),
                 pltpu.VMEM((256, 864), bf16),
-                pltpu.VMEM((2, 6, 1, 256), f32),
-                pltpu.VMEM((sizes[0] * sizes[1] - 1, 6, 1, 256), f32),
-                pltpu.VMEM((sizes[2] - 1, 6, 1, 256), f32),
-                pltpu.VMEM((1, 256), f32),
-                pltpu.VMEM((count - 1, 1, 256), f32),
+                pltpu.VMEM((2, 1, 1, 256), f32),
+                pltpu.VMEM((sizes[0] * sizes[1] - 1, 1, 1, 256), f32),
+                pltpu.VMEM((sizes[2] - 1, 1, 1, 256), f32),
+                pltpu.VMEM((2, 5, 1, 256), f32),
+                pltpu.VMEM((sizes[0] * sizes[1] - 1, 5, 1, 256), f32),
+                pltpu.VMEM((sizes[2] - 1, 5, 1, 256), f32),
+                pltpu.VMEM((HALVES, 1, WIDTH), f32),
+                pltpu.VMEM((HALVES, count - 1, 1, WIDTH), f32),
                 pltpu.SemaphoreType.DMA((4 + HALVES,)),
+                pltpu.SemaphoreType.DMA((4, HALVES)),
                 pltpu.SemaphoreType.DMA((3, HALVES)),
-                pltpu.SemaphoreType.DMA((3, HALVES)),
-                pltpu.SemaphoreType.DMA((3, HALVES)),
-                pltpu.SemaphoreType.DMA((4,)),
-                pltpu.SemaphoreType.DMA((4,)),
+                pltpu.SemaphoreType.DMA((3, HALVES, 2)),
+                pltpu.SemaphoreType.DMA((5,)),
+                pltpu.SemaphoreType.DMA((5,)),
+                pltpu.SemaphoreType.DMA((HALVES,)),
+                pltpu.SemaphoreType.DMA((HALVES,)),
             ],
             compiler_params=pltpu.CompilerParams(collective_id=0, has_side_effects=True),
         )(
@@ -514,9 +613,17 @@
             orbital_levels,
             column_shift.reshape(1, 256),
         )
-        answer = mix[0] * right_side + mix[1] * first + mix[2] * second
-        left = mix[3] * right_side + mix[4] * first + mix[5] * second + mix[6] * third
-        return answer, left
+        return pl.pallas_call(
+            combine,
+            out_shape=(out, out),
+            in_specs=[vmem] * 5,
+            out_specs=(hbm, hbm),
+            scratch_shapes=[
+                pltpu.VMEM((4, 4, 4, 4, 256), f32),
+                pltpu.VMEM((4, 4, 4, 4, 256), f32),
+                pltpu.SemaphoreType.DMA((2, 4)),
+            ],
+        )(*[pltpu.with_memory_space_constraint(value, pltpu.VMEM) for value in kept])
 
     return jax.shard_map(
         per_device,

time: 46.4 us -> 41 us (0.88)
  Pallas kernels: 42.4 us -> 40.2 us
  other arithmetic: 2.14 us -> 0 us
  local copies, waits for them, and re-layouts: 0.97 us -> 0 us
    pallas_call x1 -> x2, Pallas kernels: 42.4 us -> 40.2 us  [the longest x1 39.2 us: per_device(): pl.pallas_call(functools.partial(kernel, sizes), out_shape=(field,) * 4 +...]
    add x1 -> x0, other arithmetic: 2.14 us -> none  [per_device(): mix[3] * right_side + mix[4] * first + mix[5] * second + mix[6] * third]
    slice x1 -> x0, local copies, waits for them, and re-layouts: 0.96 us -> none  [per_device(): mix[3] * right_side + mix[4] * first + mix[5] * second + mix[6] * third]
where the time goes in v3:
time: 41 us; the launch traced here: 40.8 us
  Pallas kernels  40.2 us (98%)
  between operations  0.64 us (2%)
    pallas_call x1, Pallas kernels, per_device(): pl.pallas_call(functools.partial(kernel, sizes), out_shape=(field,) * 4 +...  39.2 us
    pallas_call x1, Pallas kernels, per_device(): pl.pallas_call(combine, out_shape=(out, out), in_specs=[vmem] * 5, out_sp...  0.97 us

profile of v3, /device:TPU:1, one launch (start us, length us, event | category | flops | bytes accessed | tf_op | source)
XLA Modules:
  0.0 40.8 jit_solution(16180080000419424606)
XLA Ops:
  0.6 39.2 %shard_map.77 = (f32[4,4,4,4,256]{4,3,2,1,0:T(4,128)S(1)}, f32[4,4,4,4,256]{4,3,2,1,0:T(4,128)S(1)}, f32[4,4,4,4,256]{4,3,2,1,0:T(4,128)S(1)}, f32[4,4,4,4,256]{4,3,2,1,0:T(4,128)S(1)}, f32[7,256]{1,0:T(8,128)S(1)}) custom-call(f32[4,4,4,4,256]{4,3,2,1,0:T(4,128)} %right_ref.1, f32[4,4,4,4,4,13]{5,4,3,2,1,0:T(4,128)} %bitcast.3, s32[4,4,4,13]{3,2,1,0:T(4,128)} %bitcast.4, ...), custom_call_target="tpu_custom_call" | custom-call | tf_op jit(solution)/shard_map/pallas_call | solution.py:568
  39.9 1.0 %shard_map.78 = (f32[4,4,4,4,256]{4,3,2,1,0:T(4,128)}, f32[4,4,4,4,256]{4,3,2,1,0:T(4,128)}) custom-call(f32[4,4,4,4,256]{4,3,2,1,0:T(4,128)S(1)} %get-tuple-element.7.zeroth_ref, f32[4,4,4,4,256]{4,3,2,1,0:T(4,128)S(1)} %get-tuple-element.8.first_ref, f32[4,4,4,4,256]{4,3,2,1,0:T(4,128)S(1)} %get-tuple-element.9.second_ref, ...), custom_call_target="tpu_custom_call" | custom-call | tf_op jit(solution)/shard_map/pallas_call | solution.py:616

commit v4 on v3

--- a/solution.py
+++ b/solution.py
@@ -136,6 +136,7 @@
     opened,
     onsite,
     levels,
+    shift,
     natural,
     flipped,
     shifted,
@@ -158,7 +159,6 @@
     halo_recv,
     other_send,
     other_recv,
-    final_send,
     final_recv,
 ):
     me = [lax.axis_index(name) for name in AXES]
@@ -188,6 +188,10 @@
         for k in range(sizes[2])
         if (i, j, k) != (0, 0, 0)
     ]
+    far = {0: 0, 1: 3, 2: 4, 3: 3, 4: 2}
+    others.sort(
+        key=lambda d: -(min(d[1], sizes[1] - d[1]) + far.get(min(d[2], sizes[2] - d[2]), 4))
+    )
 
     greeted = {tuple(d[n] % sizes[n] for n in range(3)) for d in directions}
     greeted = sorted(greeted | set(plane) | set(line))
@@ -198,14 +202,15 @@
             pltpu.make_async_copy(
                 right_ref.at[:, :, :, :, half * WIDTH : half * WIDTH + WIDTH],
                 ext.at[0, half, 1:5, 1:5, 1:5],
-                load_sem.at[half],
+                store_sem.at[half],
             )
         )
     tables = [
-        pltpu.make_async_copy(bond_ref, bonds, load_sem.at[HALVES]),
-        pltpu.make_async_copy(open_ref, opened, load_sem.at[HALVES + 1]),
-        pltpu.make_async_copy(onsite_ref, onsite, load_sem.at[HALVES + 2]),
-        pltpu.make_async_copy(level_ref, levels, load_sem.at[HALVES + 3]),
+        pltpu.make_async_copy(bond_ref, bonds, load_sem.at[0]),
+        pltpu.make_async_copy(open_ref, opened, load_sem.at[1]),
+        pltpu.make_async_copy(onsite_ref, onsite, load_sem.at[2]),
+        pltpu.make_async_copy(level_ref, levels, load_sem.at[3]),
+        pltpu.make_async_copy(shift_ref, shift, load_sem.at[4]),
     ]
     for copy in tables + loads:
         copy.start()
@@ -272,13 +277,15 @@
             outgoing[slot] = packed(hop, [shifted[k] for k in blocks])
 
     def exchange(number, half):
+        if number:
+            settle(halo_like(2), halo_send.at[half])
         for step in directions:
             part = 1 if step[2] else 0
             push(
                 ext.at[(number, half) + tuple(span_of(s, "source") for s in step)],
                 ext.at[(number, half) + tuple(span_of(s, "target") for s in step)],
-                halo_send.at[number, half],
-                halo_recv.at[number, half, part],
+                halo_send.at[half],
+                halo_recv.at[number % 2, half, part],
                 step,
             )
 
@@ -399,7 +406,7 @@
 
     def rim_times(number, half, part):
         with jax.named_scope("w_halo%d_%d" % (2 * number + half, part)):
-            settle(halo_like(part), halo_recv.at[number, half, part])
+            settle(halo_like(part), halo_recv.at[number % 2, half, part])
         rim = jnp.concatenate(
             [
                 ext[(number, half) + tuple(reach(v) for v in group)].reshape(-1, WIDTH)
@@ -409,26 +416,30 @@
         )
         return times((slice(256, 576), slice(576, 864))[part], rim)
 
-    def after(number, half):
+    def after(number, half, line_between=False):
         partial[half] = (partial[half] + rim_times(number, half, 0)) + (
             diag[...] * core(number, half)
         ).reshape(256, WIDTH)
+        if line_between:
+            to_line(1)
         total = partial[half] + rim_times(number, half, 1)
         return total.reshape(4, 4, 4, 4, WIDTH)
 
     def product(left, right):
         return jnp.sum(jnp.sum(left * right, axis=(0, 1, 2)), axis=0, keepdims=True)
 
-    stores = []
+    stores = [None] * HALVES
 
     def keep_copy(source, target, number, half):
+        if number:
+            stores[half].wait()
         copy = pltpu.make_async_copy(
             source,
             target.at[:, :, :, :, half * WIDTH : half * WIDTH + WIDTH],
-            store_sem.at[number, half],
+            store_sem.at[half],
         )
         copy.start()
-        stores.append(copy)
+        stores[half] = copy
 
     def lanes(half):
         return slice(half * WIDTH, half * WIDTH + WIDTH)
@@ -438,11 +449,12 @@
     along_line = (first_line, line_slots)
 
     def to_plane(group):
+        settle(along_line[0] if group else outgoing, other_send.at[0])
         for index, step in enumerate(plane):
             push(
                 own[group].at[0],
                 from_plane[group].at[index],
-                other_send.at[1 + group],
+                other_send.at[0],
                 other_recv.at[1 + group],
                 step,
             )
@@ -451,11 +463,12 @@
         with jax.named_scope("w_plane%d" % group):
             settle(from_plane[group], other_recv.at[1 + group])
         own[group][1] = own[group][0] + jnp.sum(from_plane[group][...], axis=0)
+        settle(from_plane[group], other_send.at[0])
         for index, step in enumerate(line):
             push(
                 own[group].at[1],
                 along_line[group].at[index],
-                other_send.at[3 + group],
+                other_send.at[0],
                 other_recv.at[3 + group],
                 step,
             )
@@ -499,32 +512,26 @@
     to_plane(1)
     g00 = from_line(0)[0]
     for half in range(HALVES):
-        last[half] = after(2, half) - GAMMA2 * core(1, half)
+        last[half] = after(2, half, half == HALVES - 1) - GAMMA2 * core(1, half)
         final_sum[half] = product(core(2, half), last[half])
+        settle(halo_like(2), halo_send.at[half])
         for index, step in enumerate(others):
             push(
                 final_sum.at[half],
                 final_slots.at[half, index],
-                final_send.at[half],
+                halo_send.at[half],
                 final_recv.at[half],
                 step,
             )
         keep_copy(last.at[half], third_ref, 3, half)
-    to_line(1)
     rest = from_line(1)
     rr2, pq, weight, start, along = early_part(
-        g00, rest[0], rest[2], rest[1], rest[3], rest[4], shift_ref[...] + CENTRE
+        g00, rest[0], rest[2], rest[1], rest[3], rest[4], shift[...] + CENTRE
     )
     with jax.named_scope("w_stores"):
         for copy in stores:
             copy.wait()
-        for number in range(3):
-            for half in range(HALVES):
-                settle(halo_like(2), halo_send.at[number, half])
-        settle(outgoing, other_send.at[0])
-        for group in range(2):
-            settle(from_plane[group], other_send.at[1 + group])
-            settle(along_line[group], other_send.at[3 + group])
+        settle(along_line[1], other_send.at[0])
     totals = []
     for half in range(HALVES):
         with jax.named_scope("w_final%d" % half):
@@ -534,7 +541,7 @@
     for n in range(7):
         mix_ref[n : n + 1, :] = start[n] + a2 * along[n]
     for half in range(HALVES):
-        settle(final_slots.at[half], final_send.at[half])
+        settle(final_slots.at[half], halo_send.at[half])
 
 
 def combine(zeroth_ref, first_ref, second_ref, third_ref, mix_ref, sol_ref, res_ref, sol, res, sem):
@@ -568,7 +575,7 @@
         kept = pl.pallas_call(
             functools.partial(kernel, sizes),
             out_shape=(field,) * 4 + (pltpu.VMEM((7, 256), f32),),
-            in_specs=[hbm] * 5 + [vmem],
+            in_specs=[hbm] * 6,
             out_specs=(hbm,) * 4 + (vmem,),
             scratch_shapes=[
                 pltpu.VMEM((3, HALVES, 6, 6, 6, 4, WIDTH), f32),
@@ -579,6 +586,7 @@
                 pltpu.VMEM((4, 4, 4, 13), jnp.int32),
                 pltpu.VMEM((4, 4, 4, 4, 4), f32),
                 pltpu.VMEM((4, 4, 4, 4), f32),
+                pltpu.VMEM((1, 256), f32),
                 pltpu.VMEM((13, 4, 256), f32),
                 pltpu.VMEM((13, 4, 256), f32),
                 pltpu.VMEM((13, 4, 256), f32),
@@ -595,13 +603,12 @@
                 pltpu.VMEM((sizes[2] - 1, 5, 1, 256), f32),
                 pltpu.VMEM((HALVES, 1, WIDTH), f32),
                 pltpu.VMEM((HALVES, count - 1, 1, WIDTH), f32),
-                pltpu.SemaphoreType.DMA((4 + HALVES,)),
-                pltpu.SemaphoreType.DMA((4, HALVES)),
-                pltpu.SemaphoreType.DMA((3, HALVES)),
-                pltpu.SemaphoreType.DMA((3, HALVES, 2)),
-                pltpu.SemaphoreType.DMA((5,)),
                 pltpu.SemaphoreType.DMA((5,)),
                 pltpu.SemaphoreType.DMA((HALVES,)),
+                pltpu.SemaphoreType.DMA((HALVES,)),
+                pltpu.SemaphoreType.DMA((2, HALVES, 2)),
+                pltpu.SemaphoreType.DMA((1,)),
+                pltpu.SemaphoreType.DMA((5,)),
                 pltpu.SemaphoreType.DMA((HALVES,)),
             ],
             compiler_params=pltpu.CompilerParams(collective_id=0, has_side_effects=True),

time: 41 us -> 39.9 us (0.973)
  Pallas kernels: 40.2 us -> 39.2 us
    pallas_call x1, Pallas kernels: 39.2 us -> 38.2 us  [per_device(): pl.pallas_call(functools.partial(kernel, sizes), out_shape=(field,) * 4 +...]
where the time goes in v4:
time: 39.9 us; the launch traced here: 39.8 us
  Pallas kernels  39.2 us (98%)
  between operations  0.64 us (2%)
    pallas_call x1, Pallas kernels, per_device(): pl.pallas_call(functools.partial(kernel, sizes), out_shape=(field,) * 4 +...  38.2 us
    pallas_call x1, Pallas kernels, per_device(): pl.pallas_call(combine, out_shape=(out, out), in_specs=[vmem] * 5, out_sp...  0.97 us

profile of v4, /device:TPU:1, one launch (start us, length us, event | category | flops | bytes accessed | tf_op | source)
XLA Modules:
  0.0 39.8 jit_solution(10960765258347414450)
XLA Ops:
  0.6 38.2 %shard_map.77 = (f32[4,4,4,4,256]{4,3,2,1,0:T(4,128)S(1)}, f32[4,4,4,4,256]{4,3,2,1,0:T(4,128)S(1)}, f32[4,4,4,4,256]{4,3,2,1,0:T(4,128)S(1)}, f32[4,4,4,4,256]{4,3,2,1,0:T(4,128)S(1)}, f32[7,256]{1,0:T(8,128)S(1)}) custom-call(f32[4,4,4,4,256]{4,3,2,1,0:T(4,128)} %right_ref.1, f32[4,4,4,4,4,13]{5,4,3,2,1,0:T(4,128)} %bitcast.3, s32[4,4,4,13]{3,2,1,0:T(4,128)} %bitcast.4, ...), custom_call_target="tpu_custom_call" | custom-call | tf_op jit(solution)/shard_map/pallas_call | solution.py:575
  38.8 1.0 %shard_map.78 = (f32[4,4,4,4,256]{4,3,2,1,0:T(4,128)}, f32[4,4,4,4,256]{4,3,2,1,0:T(4,128)}) custom-call(f32[4,4,4,4,256]{4,3,2,1,0:T(4,128)S(1)} %get-tuple-element.7.zeroth_ref, f32[4,4,4,4,256]{4,3,2,1,0:T(4,128)S(1)} %get-tuple-element.8.first_ref, f32[4,4,4,4,256]{4,3,2,1,0:T(4,128)S(1)} %get-tuple-element.9.second_ref, ...), custom_call_target="tpu_custom_call" | custom-call | tf_op jit(solution)/shard_map/pallas_call | solution.py:623

commit v5 on v4

--- a/solution.py
+++ b/solution.py
@@ -145,6 +145,7 @@
     matrix_t,
     matrix_hi,
     matrix_lo,
+    matrix_z,
     first_sum,
     first_plane,
     first_line,
@@ -189,12 +190,14 @@
         if (i, j, k) != (0, 0, 0)
     ]
     far = {0: 0, 1: 3, 2: 4, 3: 3, 4: 2}
-    others.sort(
-        key=lambda d: -(min(d[1], sizes[1] - d[1]) + far.get(min(d[2], sizes[2] - d[2]), 4))
-    )
-
+
+    def path(step):
+        return -(min(step[1], sizes[1] - step[1]) + far.get(min(step[2], sizes[2] - step[2]), 4))
+
+    others.sort(key=path)
     greeted = {tuple(d[n] % sizes[n] for n in range(3)) for d in directions}
-    greeted = sorted(greeted | set(plane) | set(line))
+    greeted = sorted(greeted | set(plane) | set(line), key=lambda d: (path(d), d))
+
 
     loads = []
     for half in range(HALVES):
@@ -276,11 +279,13 @@
         for slot, (hop, blocks) in enumerate(slabs):
             outgoing[slot] = packed(hop, [shifted[k] for k in blocks])
 
-    def exchange(number, half):
+    def exchange(number, half, parts=(1, 0)):
         if number:
             settle(halo_like(2), halo_send.at[half])
         for step in directions:
             part = 1 if step[2] else 0
+            if part not in parts:
+                continue
             push(
                 ext.at[(number, half) + tuple(span_of(s, "source") for s in step)],
                 ext.at[(number, half) + tuple(span_of(s, "target") for s in step)],
@@ -336,6 +341,13 @@
         [(place[axis] >= e - 1) & (place[axis] <= e + 1) for e in WITH_RIM]
         for axis in range(3)
     ]
+
+    def turned(chooser, span):
+        across = (((1,), (1,)), ((), ()))
+        return [
+            lax.dot_general(chooser, part, across, preferred_element_type=f32).astype(bf16)
+            for part in split(matrix_t[span, :])
+        ]
 
     def build(chosen, first_row, rows, behind):
         table = {(0, 0, 0): local}
@@ -365,15 +377,8 @@
                             both & near[2][ez + 1], table[key], 0.0
                         )
                         row += 4
-        across = (((1,), (1,)), ((), ()))
         span = slice(first_row, first_row + rows)
-        high, low = split(matrix_t[span, :])
-        matrix_hi[:, span] = lax.dot_general(
-            pick, high, across, preferred_element_type=f32
-        ).astype(bf16)
-        matrix_lo[:, span] = lax.dot_general(
-            pick, low, across, preferred_element_type=f32
-        ).astype(bf16)
+        matrix_hi[:, span], matrix_lo[:, span] = turned(pick, span)
 
     def mirrored(k, offset):
         axes = [n for n in range(3) if offset[n]]
@@ -404,26 +409,36 @@
     def before(number, half):
         partial[half] = times(slice(0, 256), core(number, half).reshape(256, WIDTH))
 
-    def rim_times(number, half, part):
+    def arrive(number, half, part):
         with jax.named_scope("w_halo%d_%d" % (2 * number + half, part)):
             settle(halo_like(part), halo_recv.at[number % 2, half, part])
+
+    def advance(number, half, target, extra, line_between=False):
+        arrive(number, half, 0)
         rim = jnp.concatenate(
             [
                 ext[(number, half) + tuple(reach(v) for v in group)].reshape(-1, WIDTH)
-                for group in (groups[1:5], groups[5:7])[part]
+                for group in groups[1:5]
             ],
             axis=0,
         )
-        return times((slice(256, 576), slice(576, 864))[part], rim)
-
-    def after(number, half, line_between=False):
-        partial[half] = (partial[half] + rim_times(number, half, 0)) + (
-            diag[...] * core(number, half)
-        ).reshape(256, WIDTH)
+        total = partial[half] + times(slice(256, 576), rim)
+        total = total.reshape(4, 4, 4, 4, WIDTH) + diag[...] * core(number, half)
+        target[...] = total if extra is None else total - extra
         if line_between:
             to_line(1)
-        total = partial[half] + rim_times(number, half, 1)
-        return total.reshape(4, 4, 4, 4, WIDTH)
+        arrive(number, half, 1)
+        for side in range(2):
+            high, low = split(ext[number, half, :, :, 5 * side].reshape(144, WIDTH))
+            part = jnp.dot(
+                matrix_z[side],
+                jnp.concatenate([low, high, high], axis=0),
+                preferred_element_type=f32,
+            )
+            target[:, :, 3 * side] += part.reshape(4, 4, 4, WIDTH)
+
+    def inner(number, half):
+        return ext.at[number, half, 1:5, 1:5, 1:5]
 
     def product(left, right):
         return jnp.sum(jnp.sum(left * right, axis=(0, 1, 2)), axis=0, keepdims=True)
@@ -490,10 +505,24 @@
     with jax.named_scope("w_coef"):
         settle(incoming, other_recv.at[0])
     with jax.named_scope("rim"):
-        build(groups[2:], 352, 512, mirrored)
-
-    for half in range(HALVES):
-        ext[1, half, 1:5, 1:5, 1:5] = after(0, half)
+        build(groups[2:], 352, 224, mirrored)
+        for side in range(2):
+            start = 576 + 144 * side
+            layer_row = out_row[0:64]
+            layer_lane = out_lane[0:64]
+            chooser = (
+                ((layer_row & 3) == (layer_lane >> 6))
+                & ((layer_row >> 2) == ((layer_lane >> 2) & 15))
+                & ((layer_lane & 3) == 3 * side)
+            )
+            high, low = turned(
+                jnp.where(chooser, 1.0, 0.0).astype(bf16), slice(start, start + 144)
+            )
+            for index, part in enumerate((high, low, high)):
+                matrix_z[side, :, 144 * index : 144 * index + 144] = part
+
+    for half in range(HALVES):
+        advance(0, half, inner(1, half), None)
         exchange(1, half)
         keep_copy(ext.at[1, half, 1:5, 1:5, 1:5], first_ref, 1, half)
         before(1, half)
@@ -502,7 +531,7 @@
         sums[0, 0, :, lanes(half)] = product(core(0, half), core(1, half))
         sums[0, 1, :, lanes(half)] = product(core(1, half), core(1, half))
     for half in range(HALVES):
-        ext[2, half, 1:5, 1:5, 1:5] = after(1, half) - GAMMA1 * core(0, half)
+        advance(1, half, inner(2, half), GAMMA1 * core(0, half))
         exchange(2, half)
         keep_copy(ext.at[2, half, 1:5, 1:5, 1:5], second_ref, 2, half)
         before(2, half)
@@ -512,7 +541,7 @@
     to_plane(1)
     g00 = from_line(0)[0]
     for half in range(HALVES):
-        last[half] = after(2, half, half == HALVES - 1) - GAMMA2 * core(1, half)
+        advance(2, half, last.at[half], GAMMA2 * core(1, half), half == HALVES - 1)
         final_sum[half] = product(core(2, half), last[half])
         settle(halo_like(2), halo_send.at[half])
         for index, step in enumerate(others):
@@ -593,8 +622,9 @@
                 pltpu.VMEM((CARGO, 4, 256), f32),
                 pltpu.VMEM((CARGO, 4, 256), f32),
                 pltpu.VMEM((864, 256), f32),
-                pltpu.VMEM((256, 864), bf16),
-                pltpu.VMEM((256, 864), bf16),
+                pltpu.VMEM((256, 576), bf16),
+                pltpu.VMEM((256, 576), bf16),
+                pltpu.VMEM((2, 64, 432), bf16),
                 pltpu.VMEM((2, 1, 1, 256), f32),
                 pltpu.VMEM((sizes[0] * sizes[1] - 1, 1, 1, 256), f32),
                 pltpu.VMEM((sizes[2] - 1, 1, 1, 256), f32),

time: 39.9 us -> 39.4 us (0.987)
  Pallas kernels: 39.2 us -> 38.6 us
    pallas_call x1, Pallas kernels: 38.2 us -> 37.6 us  [per_device(): pl.pallas_call(functools.partial(kernel, sizes), out_shape=(field,) * 4 +...]
where the time goes in v5:
time: 39.4 us; the launch traced here: 39.2 us
  Pallas kernels  38.6 us (98%)
  between operations  0.64 us (2%)
    pallas_call x1, Pallas kernels, per_device(): pl.pallas_call(functools.partial(kernel, sizes), out_shape=(field,) * 4 +...  37.6 us
    pallas_call x1, Pallas kernels, per_device(): pl.pallas_call(combine, out_shape=(out, out), in_specs=[vmem] * 5, out_sp...  0.97 us

profile of v5, /device:TPU:1, one launch (start us, length us, event | category | flops | bytes accessed | tf_op | source)
XLA Modules:
  0.0 39.2 jit_solution(1082977913861252963)
XLA Ops:
  0.6 37.6 %shard_map.77 = (f32[4,4,4,4,256]{4,3,2,1,0:T(4,128)S(1)}, f32[4,4,4,4,256]{4,3,2,1,0:T(4,128)S(1)}, f32[4,4,4,4,256]{4,3,2,1,0:T(4,128)S(1)}, f32[4,4,4,4,256]{4,3,2,1,0:T(4,128)S(1)}, f32[7,256]{1,0:T(8,128)S(1)}) custom-call(f32[4,4,4,4,256]{4,3,2,1,0:T(4,128)} %right_ref.1, f32[4,4,4,4,4,13]{5,4,3,2,1,0:T(4,128)} %bitcast.3, s32[4,4,4,13]{3,2,1,0:T(4,128)} %bitcast.4, ...), custom_call_target="tpu_custom_call" | custom-call | tf_op jit(solution)/shard_map/pallas_call | solution.py:604
  38.3 1.0 %shard_map.78 = (f32[4,4,4,4,256]{4,3,2,1,0:T(4,128)}, f32[4,4,4,4,256]{4,3,2,1,0:T(4,128)}) custom-call(f32[4,4,4,4,256]{4,3,2,1,0:T(4,128)S(1)} %get-tuple-element.7.zeroth_ref, f32[4,4,4,4,256]{4,3,2,1,0:T(4,128)S(1)} %get-tuple-element.8.first_ref, f32[4,4,4,4,256]{4,3,2,1,0:T(4,128)S(1)} %get-tuple-element.9.second_ref, ...), custom_call_target="tpu_custom_call" | custom-call | tf_op jit(solution)/shard_map/pallas_call | solution.py:653

commit v6 on v5

--- a/solution.py
+++ b/solution.py
@@ -145,6 +145,8 @@
     matrix_t,
     matrix_hi,
     matrix_lo,
+    matrix_x,
+    matrix_y,
     matrix_z,
     first_sum,
     first_plane,
@@ -163,6 +165,7 @@
     final_recv,
 ):
     me = [lax.axis_index(name) for name in AXES]
+    side_refs = (matrix_x, matrix_y, matrix_z)
 
     def at(step):
         return tuple(lax.rem(me[n] + (step[n] + sizes[n]), sizes[n]) for n in range(3))
@@ -349,7 +352,7 @@
             for part in split(matrix_t[span, :])
         ]
 
-    def build(chosen, first_row, rows, behind):
+    def build(chosen, first_row, behind):
         table = {(0, 0, 0): local}
         for k, offset in enumerate(half_offsets):
             table[offset] = flipped[k]
@@ -377,8 +380,25 @@
                             both & near[2][ez + 1], table[key], 0.0
                         )
                         row += 4
-        span = slice(first_row, first_row + rows)
-        matrix_hi[:, span], matrix_lo[:, span] = turned(pick, span)
+
+    layers = (((3, 5), (0, 0)), ((0, 0), (3, 5)), ((0, 0), (3, 5)))
+    starts = ((256, 352, 448), (448, 512, 576), (576, 720, 864))
+
+    def side_matrix(axis, side):
+        row, at_lane = out_row[0:64], out_lane[0:64]
+        x, y, z = (at_lane >> 4) & 3, (at_lane >> 2) & 3, at_lane & 3
+        along = ((y, z), (x, z), (x, y))[axis]
+        chooser = (
+            ((row & 3) == (at_lane >> 6))
+            & ((row >> 4) == along[0])
+            & (((row >> 2) & 3) == along[1])
+            & ((x, y, z)[axis] == layers[axis][side][0])
+        )
+        first, end = starts[axis][side : side + 2]
+        high, low = turned(jnp.where(chooser, 1.0, 0.0).astype(bf16), slice(first, end))
+        for index, part in enumerate((high, low, high)):
+            span = slice((end - first) * index, (end - first) * (index + 1))
+            side_refs[axis][side, :, span] = part
 
     def mirrored(k, offset):
         axes = [n for n in range(3) if offset[n]]
@@ -407,35 +427,42 @@
         return ext[number, half, 1:5, 1:5, 1:5]
 
     def before(number, half):
-        partial[half] = times(slice(0, 256), core(number, half).reshape(256, WIDTH))
+        total = times(slice(0, 256), core(number, half).reshape(256, WIDTH))
+        total = total.reshape(4, 4, 4, 4, WIDTH) + diag[...] * core(number, half)
+        if number:
+            total = total - (GAMMA1, GAMMA2)[number - 1] * core(number - 1, half)
+        partial[half] = total
 
     def arrive(number, half, part):
         with jax.named_scope("w_halo%d_%d" % (2 * number + half, part)):
             settle(halo_like(part), halo_recv.at[number % 2, half, part])
 
-    def advance(number, half, target, extra, line_between=False):
+    def advance(number, half, target):
+        def add(axis):
+            for side in range(2):
+                out, rim = layers[axis][side]
+                where = [slice(None)] * 3
+                where[axis] = out
+                if axis == 0:
+                    value = ext[number, half, rim, :, 1:5]
+                elif axis == 1:
+                    value = ext[number, half, 1:5, rim, 1:5]
+                else:
+                    value = ext[number, half, :, :, rim]
+                high, low = split(value.reshape(-1, WIDTH))
+                part = jnp.dot(
+                    side_refs[axis][side],
+                    jnp.concatenate([low, high, high], axis=0),
+                    preferred_element_type=f32,
+                )
+                target[tuple(where)] += part.reshape(4, 4, 4, WIDTH)
+
+        target[...] = partial[half]
         arrive(number, half, 0)
-        rim = jnp.concatenate(
-            [
-                ext[(number, half) + tuple(reach(v) for v in group)].reshape(-1, WIDTH)
-                for group in groups[1:5]
-            ],
-            axis=0,
-        )
-        total = partial[half] + times(slice(256, 576), rim)
-        total = total.reshape(4, 4, 4, 4, WIDTH) + diag[...] * core(number, half)
-        target[...] = total if extra is None else total - extra
-        if line_between:
-            to_line(1)
+        add(0)
+        add(1)
         arrive(number, half, 1)
-        for side in range(2):
-            high, low = split(ext[number, half, :, :, 5 * side].reshape(144, WIDTH))
-            part = jnp.dot(
-                matrix_z[side],
-                jnp.concatenate([low, high, high], axis=0),
-                preferred_element_type=f32,
-            )
-            target[:, :, 3 * side] += part.reshape(4, 4, 4, WIDTH)
+        add(2)
 
     def inner(number, half):
         return ext.at[number, half, 1:5, 1:5, 1:5]
@@ -496,7 +523,9 @@
     for half in range(HALVES):
         keep_copy(ext.at[0, half, 1:5, 1:5, 1:5], zeroth_ref, 0, half)
     with jax.named_scope("inner"):
-        build(groups[:2], 0, 352, lambda k, offset: shifted[k])
+        build(groups[:2], 0, lambda k, offset: shifted[k])
+        matrix_hi[...], matrix_lo[...] = turned(pick, slice(0, 256))
+        side_matrix(0, 0)
         for half in range(HALVES):
             before(0, half)
     for half in range(HALVES):
@@ -505,24 +534,12 @@
     with jax.named_scope("w_coef"):
         settle(incoming, other_recv.at[0])
     with jax.named_scope("rim"):
-        build(groups[2:], 352, 224, mirrored)
-        for side in range(2):
-            start = 576 + 144 * side
-            layer_row = out_row[0:64]
-            layer_lane = out_lane[0:64]
-            chooser = (
-                ((layer_row & 3) == (layer_lane >> 6))
-                & ((layer_row >> 2) == ((layer_lane >> 2) & 15))
-                & ((layer_lane & 3) == 3 * side)
-            )
-            high, low = turned(
-                jnp.where(chooser, 1.0, 0.0).astype(bf16), slice(start, start + 144)
-            )
-            for index, part in enumerate((high, low, high)):
-                matrix_z[side, :, 144 * index : 144 * index + 144] = part
-
-    for half in range(HALVES):
-        advance(0, half, inner(1, half), None)
+        build(groups[2:], 352, mirrored)
+        for axis, side in ((0, 1), (1, 0), (1, 1), (2, 0), (2, 1)):
+            side_matrix(axis, side)
+
+    for half in range(HALVES):
+        advance(0, half, inner(1, half))
         exchange(1, half)
         keep_copy(ext.at[1, half, 1:5, 1:5, 1:5], first_ref, 1, half)
         before(1, half)
@@ -531,7 +548,7 @@
         sums[0, 0, :, lanes(half)] = product(core(0, half), core(1, half))
         sums[0, 1, :, lanes(half)] = product(core(1, half), core(1, half))
     for half in range(HALVES):
-        advance(1, half, inner(2, half), GAMMA1 * core(0, half))
+        advance(1, half, inner(2, half))
         exchange(2, half)
         keep_copy(ext.at[2, half, 1:5, 1:5, 1:5], second_ref, 2, half)
         before(2, half)
@@ -541,10 +558,12 @@
     to_plane(1)
     g00 = from_line(0)[0]
     for half in range(HALVES):
-        advance(2, half, last.at[half], GAMMA2 * core(1, half), half == HALVES - 1)
+        advance(2, half, last.at[half])
         final_sum[half] = product(core(2, half), last[half])
         settle(halo_like(2), halo_send.at[half])
         for index, step in enumerate(others):
+            if half == HALVES - 1 and index == 60:
+                to_line(1)
             push(
                 final_sum.at[half],
                 final_slots.at[half, index],
@@ -574,22 +593,19 @@
 
 
 def combine(zeroth_ref, first_ref, second_ref, third_ref, mix_ref, sol_ref, res_ref, sol, res, sem):
-    copies = []
-    for x in range(4):
-        zeroth, first, second = zeroth_ref[x], first_ref[x], second_ref[x]
-        sol[x] = mix_ref[0] * zeroth + mix_ref[1] * first + mix_ref[2] * second
-        res[x] = (
+    for part in [(slice(x, x + 1), slice(y, y + 2)) for x in range(4) for y in (0, 2)]:
+        zeroth, first, second = zeroth_ref[part], first_ref[part], second_ref[part]
+        res[part] = (
             mix_ref[3] * zeroth
             + mix_ref[4] * first
             + mix_ref[5] * second
-            + mix_ref[6] * third_ref[x]
-        )
-        copies.append(pltpu.make_async_copy(sol.at[x], sol_ref.at[x], sem.at[0, x]))
-        copies.append(pltpu.make_async_copy(res.at[x], res_ref.at[x], sem.at[1, x]))
-        for copy in copies[-2:]:
-            copy.start()
-    for copy in copies:
-        copy.wait()
+            + mix_ref[6] * third_ref[part]
+        )
+        pltpu.make_async_copy(res.at[part], res_ref.at[part], sem.at[1]).start()
+        sol[part] = mix_ref[0] * zeroth + mix_ref[1] * first + mix_ref[2] * second
+        pltpu.make_async_copy(sol.at[part], sol_ref.at[part], sem.at[0]).start()
+    pltpu.make_async_copy(sol, sol_ref, sem.at[0]).wait()
+    pltpu.make_async_copy(res, res_ref, sem.at[1]).wait()
 
 
 def solution(mesh):
@@ -609,7 +625,7 @@
             scratch_shapes=[
                 pltpu.VMEM((3, HALVES, 6, 6, 6, 4, WIDTH), f32),
                 pltpu.VMEM((HALVES, 4, 4, 4, 4, WIDTH), f32),
-                pltpu.VMEM((HALVES, 256, WIDTH), f32),
+                pltpu.VMEM((HALVES, 4, 4, 4, 4, WIDTH), f32),
                 pltpu.VMEM((4, 4, 4, 4, WIDTH), f32),
                 pltpu.VMEM((4, 4, 4, 4, 4, 13), f32),
                 pltpu.VMEM((4, 4, 4, 13), jnp.int32),
@@ -622,8 +638,10 @@
                 pltpu.VMEM((CARGO, 4, 256), f32),
                 pltpu.VMEM((CARGO, 4, 256), f32),
                 pltpu.VMEM((864, 256), f32),
-                pltpu.VMEM((256, 576), bf16),
-                pltpu.VMEM((256, 576), bf16),
+                pltpu.VMEM((256, 256), bf16),
+                pltpu.VMEM((256, 256), bf16),
+                pltpu.VMEM((2, 64, 288), bf16),
+                pltpu.VMEM((2, 64, 192), bf16),
                 pltpu.VMEM((2, 64, 432), bf16),
                 pltpu.VMEM((2, 1, 1, 256), f32),
                 pltpu.VMEM((sizes[0] * sizes[1] - 1, 1, 1, 256), f32),
@@ -658,7 +676,7 @@
             scratch_shapes=[
                 pltpu.VMEM((4, 4, 4, 4, 256), f32),
                 pltpu.VMEM((4, 4, 4, 4, 256), f32),
-                pltpu.SemaphoreType.DMA((2, 4)),
+                pltpu.SemaphoreType.DMA((2,)),
             ],
         )(*[pltpu.with_memory_space_constraint(value, pltpu.VMEM) for value in kept])
 

time: 39.4 us -> 39.2 us (level)
  no operation moved by 1% of the time
where the time goes in v6:
time: 39.2 us; the launch traced here: 39.1 us
  Pallas kernels  38.4 us (98%)
  between operations  0.64 us (2%)
    pallas_call x1, Pallas kernels, per_device(): pl.pallas_call(functools.partial(kernel, sizes), out_shape=(field,) * 4 +...  37.5 us
    pallas_call x1, Pallas kernels, per_device(): pl.pallas_call(combine, out_shape=(out, out), in_specs=[vmem] * 5, out_sp...  0.9 us

profile of v6, /device:TPU:1, one launch (start us, length us, event | category | flops | bytes accessed | tf_op | source)
XLA Modules:
  0.0 39.1 jit_solution(4854823105704827544)
XLA Ops:
  0.6 37.5 %shard_map.77 = (f32[4,4,4,4,256]{4,3,2,1,0:T(4,128)S(1)}, f32[4,4,4,4,256]{4,3,2,1,0:T(4,128)S(1)}, f32[4,4,4,4,256]{4,3,2,1,0:T(4,128)S(1)}, f32[4,4,4,4,256]{4,3,2,1,0:T(4,128)S(1)}, f32[7,256]{1,0:T(8,128)S(1)}) custom-call(f32[4,4,4,4,256]{4,3,2,1,0:T(4,128)} %right_ref.1, f32[4,4,4,4,4,13]{5,4,3,2,1,0:T(4,128)} %bitcast.3, s32[4,4,4,13]{3,2,1,0:T(4,128)} %bitcast.4, ...), custom_call_target="tpu_custom_call" | custom-call | tf_op jit(solution)/shard_map/pallas_call | solution.py:620
  38.2 0.9 %shard_map.78 = (f32[4,4,4,4,256]{4,3,2,1,0:T(4,128)}, f32[4,4,4,4,256]{4,3,2,1,0:T(4,128)}) custom-call(f32[4,4,4,4,256]{4,3,2,1,0:T(4,128)S(1)} %get-tuple-element.7.zeroth_ref, f32[4,4,4,4,256]{4,3,2,1,0:T(4,128)S(1)} %get-tuple-element.8.first_ref, f32[4,4,4,4,256]{4,3,2,1,0:T(4,128)S(1)} %get-tuple-element.9.second_ref, ...), custom_call_target="tpu_custom_call" | custom-call | tf_op jit(solution)/shard_map/pallas_call | solution.py:671

commit v7 on v6

--- a/solution.py
+++ b/solution.py
@@ -270,10 +270,10 @@
         blocks = bonds[...] * opened[...].astype(f32)
         table = blocks.reshape(1024, 13).T
         for orb in range(4):
-            natural[:, orb, :] = table[:, 256 * orb : 256 * orb + 256]
+            natural[0:13, orb, :] = table[:, 256 * orb : 256 * orb + 256]
         table = jnp.swapaxes(blocks, 0, 1).reshape(1024, 13).T
         for orb in range(4):
-            flipped[:, orb, :] = table[:, 256 * orb : 256 * orb + 256]
+            flipped[0:13, orb, :] = table[:, 256 * orb : 256 * orb + 256]
         for k, offset in enumerate(half_offsets):
             value = natural[k]
             for axis in range(3):
@@ -632,9 +632,9 @@
                 pltpu.VMEM((4, 4, 4, 4, 4), f32),
                 pltpu.VMEM((4, 4, 4, 4), f32),
                 pltpu.VMEM((1, 256), f32),
-                pltpu.VMEM((13, 4, 256), f32),
-                pltpu.VMEM((13, 4, 256), f32),
-                pltpu.VMEM((13, 4, 256), f32),
+                pltpu.VMEM((16, 4, 256), f32),
+                pltpu.VMEM((16, 4, 256), f32),
+                pltpu.VMEM((16, 4, 256), f32),
                 pltpu.VMEM((CARGO, 4, 256), f32),
                 pltpu.VMEM((CARGO, 4, 256), f32),
                 pltpu.VMEM((864, 256), f32),

time: 39.2 us -> 39.2 us (level)
  no operation moved by 1% of the time
where the time goes in v7:
time: 39.2 us; the launch traced here: 39.1 us
  Pallas kernels  38.4 us (98%)
  between operations  0.64 us (2%)
    pallas_call x1, Pallas kernels, per_device(): pl.pallas_call(functools.partial(kernel, sizes), out_shape=(field,) * 4 +...  37.5 us
    pallas_call x1, Pallas kernels, per_device(): pl.pallas_call(combine, out_shape=(out, out), in_specs=[vmem] * 5, out_sp...  0.9 us

profile of v7, /device:TPU:1, one launch (start us, length us, event | category | flops | bytes accessed | tf_op | source)
XLA Modules:
  0.0 39.1 jit_solution(16855552393423508537)
XLA Ops:
  0.6 37.5 %shard_map.77 = (f32[4,4,4,4,256]{4,3,2,1,0:T(4,128)S(1)}, f32[4,4,4,4,256]{4,3,2,1,0:T(4,128)S(1)}, f32[4,4,4,4,256]{4,3,2,1,0:T(4,128)S(1)}, f32[4,4,4,4,256]{4,3,2,1,0:T(4,128)S(1)}, f32[7,256]{1,0:T(8,128)S(1)}) custom-call(f32[4,4,4,4,256]{4,3,2,1,0:T(4,128)} %right_ref.1, f32[4,4,4,4,4,13]{5,4,3,2,1,0:T(4,128)} %bitcast.3, s32[4,4,4,13]{3,2,1,0:T(4,128)} %bitcast.4, ...), custom_call_target="tpu_custom_call" | custom-call | tf_op jit(solution)/shard_map/pallas_call | solution.py:620
  38.2 0.9 %shard_map.78 = (f32[4,4,4,4,256]{4,3,2,1,0:T(4,128)}, f32[4,4,4,4,256]{4,3,2,1,0:T(4,128)}) custom-call(f32[4,4,4,4,256]{4,3,2,1,0:T(4,128)S(1)} %get-tuple-element.7.zeroth_ref, f32[4,4,4,4,256]{4,3,2,1,0:T(4,128)S(1)} %get-tuple-element.8.first_ref, f32[4,4,4,4,256]{4,3,2,1,0:T(4,128)S(1)} %get-tuple-element.9.second_ref, ...), custom_call_target="tpu_custom_call" | custom-call | tf_op jit(solution)/shard_map/pallas_call | solution.py:671

commit v8 on v7

--- a/solution.py
+++ b/solution.py
@@ -306,9 +306,8 @@
         count = sum(1 for slab in slabs if slab[0] == hop)
         rows = slice(cargo_start[hop], cargo_start[hop] + count)
         push(outgoing.at[rows], incoming.at[rows], other_send.at[0], other_recv.at[0], hop)
-    for half in range(HALVES):
-        loads[half].wait()
-        exchange(0, half)
+    loads[0].wait()
+    exchange(0, 0)
 
     out_row = lax.broadcasted_iota(jnp.int32, (256, 256), 0)
     out_lane = lax.broadcasted_iota(jnp.int32, (256, 256), 1)
@@ -339,6 +338,10 @@
         level = jnp.sum(jnp.where(keep, wide, 0.0), axis=0, keepdims=True)
         level = jnp.sum(jnp.where(same, level, 0.0), axis=1, keepdims=True)
         diag[...] = jnp.broadcast_to(level, (256, WIDTH)).reshape(4, 4, 4, 4, WIDTH)
+
+    for half in range(1, HALVES):
+        loads[half].wait()
+        exchange(0, half)
 
     near = [
         [(place[axis] >= e - 1) & (place[axis] <= e + 1) for e in WITH_RIM]

time: 39.2 us -> 39.2 us (level)
  no operation moved by 1% of the time
where the time goes in v8:
time: 39.2 us; the launch traced here: 39.1 us
  Pallas kernels  38.4 us (98%)
  between operations  0.64 us (2%)
    pallas_call x1, Pallas kernels, per_device(): pl.pallas_call(functools.partial(kernel, sizes), out_shape=(field,) * 4 +...  37.5 us
    pallas_call x1, Pallas kernels, per_device(): pl.pallas_call(combine, out_shape=(out, out), in_specs=[vmem] * 5, out_sp...  0.9 us

profile of v8, /device:TPU:1, one launch (start us, length us, event | category | flops | bytes accessed | tf_op | source)
XLA Modules:
  0.0 39.1 jit_solution(2710832735570570500)
XLA Ops:
  0.6 37.5 %shard_map.77 = (f32[4,4,4,4,256]{4,3,2,1,0:T(4,128)S(1)}, f32[4,4,4,4,256]{4,3,2,1,0:T(4,128)S(1)}, f32[4,4,4,4,256]{4,3,2,1,0:T(4,128)S(1)}, f32[4,4,4,4,256]{4,3,2,1,0:T(4,128)S(1)}, f32[7,256]{1,0:T(8,128)S(1)}) custom-call(f32[4,4,4,4,256]{4,3,2,1,0:T(4,128)} %right_ref.1, f32[4,4,4,4,4,13]{5,4,3,2,1,0:T(4,128)} %bitcast.3, s32[4,4,4,13]{3,2,1,0:T(4,128)} %bitcast.4, ...), custom_call_target="tpu_custom_call" | custom-call | tf_op jit(solution)/shard_map/pallas_call | solution.py:623
  38.2 0.9 %shard_map.78 = (f32[4,4,4,4,256]{4,3,2,1,0:T(4,128)}, f32[4,4,4,4,256]{4,3,2,1,0:T(4,128)}) custom-call(f32[4,4,4,4,256]{4,3,2,1,0:T(4,128)S(1)} %get-tuple-element.7.zeroth_ref, f32[4,4,4,4,256]{4,3,2,1,0:T(4,128)S(1)} %get-tuple-element.8.first_ref, f32[4,4,4,4,256]{4,3,2,1,0:T(4,128)S(1)} %get-tuple-element.9.second_ref, ...), custom_call_target="tpu_custom_call" | custom-call | tf_op jit(solution)/shard_map/pallas_call | solution.py:674
